TPU v7x, 32 devices: a whole 2x2x4 slice. The times are simulated.
32 devices in a mesh: act: 4 (over y, x), virt: 8 (over z, core).
Axes of the slice: x: 2, y: 2, z: 4, core: 2. Of those that a mesh axis runs over, the one named last changes fastest.
Arguments:
- amplitudes: bfloat16 [400, 640, 640], P('act', 'virt'), may hold values from -6 to 6
- virtual_fock_block: bfloat16 [640, 640], replicated, may hold values from -1 to 3.1, as said below
- metric: bfloat16 [400, 400], replicated, may hold values from -3.5 to 3.5, as said below
- active_block: bfloat16 [400, 400], replicated, may hold values from -0.3125 to 0.3125
Outputs:
- residual_vec: bfloat16 [400, 640, 640], P('act', 'virt')
- rayleigh: float32 [], replicated
- res_norm: float32 [], replicated
Inputs may be any that keep to these rules, and one draw needn't show every extreme that they name: `virtual_fock_block`: symmetric. `metric`: symmetric positive definite.
All inputs are finite; a program needn't handle non-finite values.
Results may differ from a plain program's by a relative error of at most 0.0099.
Values may be sent and summed in bfloat16 or wider, within the bound.
A program may use at most 192 MiB of HBM per device.

v0:
```python
import jax
import jax.numpy as jnp
from jax import lax
from jax.sharding import PartitionSpec as P


def fock_apply(operator, piece):
    rows = piece.shape[0]
    flat_piece = piece.reshape(rows, -1)
    product = jnp.dot(operator, flat_piece, preferred_element_type=jnp.float32)
    return product.astype(jnp.bfloat16).reshape(piece.shape)


def local(amplitudes, virtual_fock_block, metric, active_block):
    trial_rows = lax.all_to_all(amplitudes, "act", split_axis=1, concat_axis=0, tiled=True)
    pair_count, row_count, item_count = trial_rows.shape
    flat_trial = trial_rows.reshape(pair_count, row_count * item_count)
    weighted_rows = jnp.einsum("vq,tv->qt", flat_trial, metric, preferred_element_type=jnp.float32)
    active_rows = jnp.einsum(
        "vq,tv->qt", flat_trial, active_block, preferred_element_type=jnp.float32
    )
    halved_rows = weighted_rows.astype(jnp.bfloat16)
    turned_trial = jnp.transpose(flat_trial)
    shape_abt = (row_count, item_count, pair_count)
    trial_rows, weighted_rows, halved_rows, active_rows = (
        turned_trial.reshape(shape_abt),
        weighted_rows.reshape(shape_abt),
        halved_rows.reshape(shape_abt),
        active_rows.reshape(shape_abt),
    )
    virt_count = lax.axis_size("virt")
    act_count = lax.axis_size("act")
    sub_rows = virtual_fock_block.shape[0] // (virt_count * act_count)
    width = virtual_fock_block.shape[0]
    permuted = (
        virtual_fock_block.reshape(virt_count, act_count, sub_rows, width)
        .transpose(1, 0, 2, 3)
        .reshape(width, width)
    )
    permuted = (
        permuted.reshape(width, virt_count, act_count, sub_rows)
        .transpose(0, 2, 1, 3)
        .reshape(width, width)
    )
    product = fock_apply(
        permuted,
        lax.all_to_all(halved_rows, ("act", "virt"), split_axis=1, concat_axis=0, tiled=True),
    )
    left_portion = lax.all_to_all(product, ("act", "virt"), split_axis=0, concat_axis=1, tiled=True)
    right_part = jnp.einsum(
        "cb,act->abt", virtual_fock_block, halved_rows, preferred_element_type=jnp.float32
    )
    sigma_rows = left_portion.astype(jnp.float32) + right_part + active_rows
    trial_wide = trial_rows.astype(jnp.float32)
    numer_local = jnp.sum(trial_wide * sigma_rows)
    denom_local = jnp.sum(trial_wide * weighted_rows)
    numerator, denominator = lax.psum((numer_local, denom_local), ("act", "virt"))
    rayleigh = numerator / denominator
    resid = sigma_rows - rayleigh * weighted_rows
    squares_total = lax.psum(jnp.sum(resid * resid), ("act", "virt"))
    res_norm = squares_total / denominator
    returned = lax.all_to_all(
        resid.astype(jnp.bfloat16), "act", split_axis=2, concat_axis=0, tiled=True
    )
    residual_vec = jnp.transpose(returned, (2, 0, 1))
    return (residual_vec, rayleigh, res_norm)


def solution(mesh):
    placed = (P("act", "virt", None), P(), P(), P())
    return jax.shard_map(
        local,
        mesh=mesh,
        in_specs=placed,
        out_specs=(P("act", "virt", None), P(), P()),
        check_vma=False,
    )
```

profile of v0, /device:TPU:0, one launch (start us, length us, event | category | flops | bytes accessed | tf_op | source)
XLA Modules:
  0.0 1439.3 jit_solution(7512627883030693005)
XLA Ops:
  0.6 7.3 copy.67
  7.9 122.3 %all_to_all.57 = bf16[100,80,640]{2,0,1:T(8,128)(2,1)S(1)} all-to-all(bf16[100,80,640]{2,0,1:T(8,128)(2,1)S(1)} %copy.67), channel_id=1, replica_groups=mesh['act'=4,'virt'=8] {'act'}, dimensions={1} | all-to-all | bytes 20480000 | tf_op jit(solution)/shard_map/all_to_all | solution.py:15
  130.2 4.5 copy.68
  134.8 4.5 copy-done.2
  139.2 4.7 copy.94
  143.9 20.2 %multiply_reduce_fusion.1 = (f32[]{:T(128)}, bf16[12800,400]{0,1:T(8,128)(2,1)}, f32[12800,400]{0,1:T(8,128)}) fusion(bf16[400,12800]{1,0:T(8,128)(2,1)} %bitcast.86, bf16[400,400]{1,0:T(8,128)(2,1)S(1)} %copy-done), kind=kOutput, calls=%fused_computation.4 | convolution fusion | flops 4116480000 | bytes 41280004 | tf_op jit(solution)/shard_map/vq,tv->qt/dot_general | solution.py:18
  164.1 16.3 %reshape.37 = bf16[20,640,400]{1,0,2:T(8,128)(2,1)} reshape(bf16[12800,400]{0,1:T(8,128)(2,1)} %get-tuple-element.20) | data formatting | bytes 20480000 | tf_op jit(solution)/shard_map/reshape | solution.py:28
  180.5 21.7 %copy.69 = bf16[20,640,400]{2,0,1:T(8,128)(2,1)} copy(bf16[20,640,400]{1,0,2:T(8,128)(2,1)} %reshape.37) | data formatting | bytes 20480000 | tf_op jit(solution)/shard_map/reshape | solution.py:28
  206.7 4.7 copy.72
  211.5 10.2 reshape_reshape.3
  221.9 326.5 %all-to-all-done.1 = bf16[20,640,400]{2,0,1:T(8,128)(2,1)} async-done(((bf16[20,640,400]{2,0,1:T(8,128)(2,1)}), bf16[20,640,400]{2,0,1:T(8,128)(2,1)}, u32[]{:S(2)}, u32[]{:S(2)}) %all-to-all-start.1) | async-done | bytes 10240032 | tf_op jit(solution)/shard_map/all_to_all | solution.py:47
  548.5 16.1 %copy.71 = bf16[32,20,20,400]{3,2,1,0:T(8,128)(2,1)} copy(bf16[32,20,20,400]{3,1,2,0:T(8,128)(2,1)} %bitcast.4) | data formatting | bytes 20480000 | tf_op jit(solution)/shard_map/all_to_all | solution.py:47
  564.6 24.1 %reshape.38 = bf16[640,8000]{1,0:T(8,128)(2,1)} reshape(bf16[32,20,20,400]{3,2,1,0:T(8,128)(2,1)} %copy.71) | data formatting | bytes 20480000 | tf_op jit(solution)/shard_map/reshape | solution.py:9
  588.7 15.5 %convolution_convert_fusion = bf16[8000,640]{1,0:T(8,128)(2,1)} fusion(bf16[640,8000]{1,0:T(8,128)(2,1)} %reshape.38, bf16[640,640]{0,1:T(8,128)(2,1)S(1)} %reshape.40), kind=kOutput, calls=%fused_computation.6 | convolution fusion | flops 6558720000 | bytes 21299200 | tf_op jit(solution)/shard_map/dot_general | solution.py:10
  604.2 20.7 %copy.74 = bf16[640,20,400]{2,1,0:T(8,128)(2,1)} copy(bf16[640,20,400]{0,2,1:T(8,128)(2,1)} %bitcast.87) | data formatting | bytes 20480000 | tf_op jit(solution)/shard_map/reshape | solution.py:11
  629.1 15.1 %fusion.1 = f32[20,640,400]{1,2,0:T(8,128)} fusion(bf16[400,400]{1,0:T(8,128)(2,1)S(1)} %copy-done.4, bf16[50,8,20,640]{3,2,1,0:T(8,128)(2,1)} %bitcast.77), kind=kOutput, calls=%fused_computation.7 | convolution fusion | flops 4096000000 | bytes 31040000 | tf_op jit(solution)/shard_map/vq,tv->qt/dot_general | solution.py:19
  644.2 326.7 %all-to-all-done.2 = bf16[640,20,400]{2,1,0:T(8,128)(2,1)} async-done(((bf16[640,20,400]{2,1,0:T(8,128)(2,1)}), bf16[640,20,400]{2,1,0:T(8,128)(2,1)}, u32[]{:S(2)}, u32[]{:S(2)}) %all-to-all-start.2) | async-done | bytes 10240032 | tf_op jit(solution)/shard_map/all_to_all | solution.py:49
  971.0 19.0 %copy.75 = bf16[640,20,400]{0,2,1:T(8,128)(2,1)} copy(bf16[640,20,400]{2,1,0:T(8,128)(2,1)} %all-to-all-done.2) | data formatting | bytes 20480000 | tf_op jit(solution)/shard_map/all_to_all | solution.py:49
  990.0 18.8 %copy.76 = f32[640,20,400]{2,0,1:T(8,128)} copy(bf16[640,20,400]{0,2,1:T(8,128)(2,1)} %copy.75) | data formatting | bytes 30720000 | tf_op jit(solution)/shard_map/convert_element_type | solution.py:53
  1008.8 29.6 %reshape.43 = f32[32,20,20,400]{3,1,0,2:T(8,128)} reshape(f32[640,20,400]{2,0,1:T(8,128)} %copy.76) | data formatting | bytes 40960000 | tf_op jit(solution)/shard_map/convert_element_type | solution.py:53
  1038.4 28.7 %copy.77 = f32[20,32,20,400]{3,2,1,0:T(8,128)} copy(f32[20,32,20,400]{3,0,1,2:T(8,128)} %bitcast.82) | data formatting | bytes 40960000 | tf_op jit(solution)/shard_map/convert_element_type | solution.py:53
  1067.1 30.1 %reshape.42 = f32[20,640,400]{2,1,0:T(8,128)} reshape(f32[20,32,20,400]{3,2,1,0:T(8,128)} %copy.77) | data formatting | bytes 40960000 | tf_op jit(solution)/shard_map/convert_element_type | solution.py:53
  1097.2 25.1 %copy.79 = f32[20,640,400]{1,2,0:T(8,128)} copy(f32[20,640,400]{2,1,0:T(8,128)} %reshape.42) | data formatting | bytes 40960000 | tf_op jit(solution)/shard_map/convert_element_type | solution.py:53
  1122.3 35.7 %multiply_reduce_fusion.2 = (f32[]{:T(128)}, f32[20,640,400]{1,2,0:T(8,128)}) fusion(f32[20,640,400]{1,2,0:T(8,128)} %fusion.1, f32[20,640,400]{1,2,0:T(8,128)} %copy.79, bf16[640,640]{1,0:T(8,128)(2,1)S(1)} %copy-done.3, bf16[50,20,8,640]{3,2,1,0:T(8,128)(2,1)} %bitcast.79, bf16[50,8,20,640]{3,2,1,0:T(8,128)(2,1)} %bitcast.78), kind=kOutput, calls=%fused_computation.5 | convolution fusion | flops 6579200000 | bytes 82739200 | tf_op jit(solution)/shard_map/cb,act->abt/dot_general | solution.py:50
  1158.0 37.3 %all-reduce = (f32[]{:T(128)}, f32[]{:T(128)}) all-reduce(f32[]{:T(128)} %get-tuple-element.22, f32[]{:T(128)} %get-tuple-element.19), channel_id=1, replica_groups=mesh['act'=4,'virt'=8] {'act','virt'}, use_global_device_ids=true, to_apply=%region_1.0 | all-reduce | flops 2 | bytes 16 | tf_op jit(solution)/shard_map/psum | solution.py:57
  1196.7 17.7 %broadcast_multiply_fusion = f32[12800,400]{0,1:T(8,128)} fusion(f32[12800,400]{0,1:T(8,128)} %get-tuple-element.21, f32[]{:T(128)} %div.6), kind=kLoop, calls=%fused_computation.12 | loop fusion | flops 5120000 | bytes 40960004 | tf_op jit(solution)/shard_map/mul | solution.py:59
  1216.9 10.6 multiply_reduce_fusion
  1227.5 14.1 copy.83
  1241.6 6.3 all-to-all-start.3
  1247.9 166.9 %psum.23 = f32[]{:T(128)} all-reduce(f32[]{:T(128)} %get-tuple-element.17), channel_id=1, replica_groups=mesh['act'=4,'virt'=8] {'act','virt'}, use_global_device_ids=true, to_apply=%region_5.0 | all-reduce | flops 1 | bytes 8 | tf_op jit(solution)/shard_map/psum | solution.py:60
  1416.1 11.6 copy.85
  1427.7 9.3 copy.86
  (26 shorter events, 11.5 us)
Async XLA Ops:
  0.6 143.3 %copy-start = (bf16[400,400]{1,0:T(8,128)(2,1)S(1)}, bf16[400,400]{1,0:T(8,128)(2,1)}, u32[]{:S(2)}) copy-start(bf16[400,400]{1,0:T(8,128)(2,1)} %param.6) | copy-start | bytes 960004
  134.7 4.5 copy-start.2
  202.2 4.4 copy-start.3
  202.2 346.3 %all-to-all-start.1 = ((bf16[20,640,400]{2,0,1:T(8,128)(2,1)}), bf16[20,640,400]{2,0,1:T(8,128)(2,1)}, u32[]{:S(2)}, u32[]{:S(2)}) async-start(bf16[20,640,400]{2,0,1:T(8,128)(2,1)} %copy.69), calls=%async_computation.1 | async-start | bytes 31457280 | tf_op jit(solution)/shard_map/all_to_all | solution.py:47
  624.9 4.2 copy-start.4
  624.9 346.1 %all-to-all-start.2 = ((bf16[640,20,400]{2,1,0:T(8,128)(2,1)}), bf16[640,20,400]{2,1,0:T(8,128)(2,1)}, u32[]{:S(2)}, u32[]{:S(2)}) async-start(bf16[640,20,400]{2,1,0:T(8,128)(2,1)} %copy.74), calls=%async_computation.2 | async-start | bytes 31457280 | tf_op jit(solution)/shard_map/all_to_all | solution.py:49
  1196.7 17.7 %slice-start = ((s8[20480000]{0:T(1024)(128)(4,1)}), s8[4194304]{0:T(1024)(128)(4,1)S(1)}, s32[]{:S(2)}) async-start(s8[20480000]{0:T(1024)(128)(4,1)} %bitcast.80), calls=%async_computation.4 | async-start | bytes 8388608
  1196.7 17.7 %slice-start.1 = ((s8[20480000]{0:T(1024)(128)(4,1)}), s8[4194304]{0:T(1024)(128)(4,1)S(1)}, s32[]{:S(2)}) async-start(s8[20480000]{0:T(1024)(128)(4,1)} %bitcast.80), calls=%async_computation.5 | async-start | bytes 8388608
  1196.7 17.7 %slice-start.2 = ((s8[20480000]{0:T(1024)(128)(4,1)}), s8[4194304]{0:T(1024)(128)(4,1)S(1)}, s32[]{:S(2)}) async-start(s8[20480000]{0:T(1024)(128)(4,1)} %bitcast.80), calls=%async_computation.6 | async-start | bytes 8388608
  1196.7 19.1 %slice-start.3 = ((s8[20480000]{0:T(1024)(128)(4,1)}), s8[4194304]{0:T(1024)(128)(4,1)S(1)}, s32[]{:S(2)}) async-start(s8[20480000]{0:T(1024)(128)(4,1)} %bitcast.80), calls=%async_computation.7 | async-start | bytes 8388608
  1196.7 20.2 %slice-start.4 = ((s8[20480000]{0:T(1024)(128)(4,1)}), s8[3702784]{0:T(1024)(128)(4,1)S(1)}, s32[]{:S(2)}) async-start(s8[20480000]{0:T(1024)(128)(4,1)} %bitcast.80), calls=%async_computation.8 | async-start | bytes 7405568
  1241.6 174.5 %all-to-all-start.3 = ((bf16[20,640,400]{1,0,2:T(8,128)(2,1)}), bf16[20,640,400]{1,0,2:T(8,128)(2,1)}, u32[]{:S(2)}, u32[]{:S(2)}) async-start(bf16[20,640,400]{1,0,2:T(8,128)(2,1)} %copy.83), calls=%async_computation.3 | async-start | bytes 24576000 | tf_op jit(solution)/shard_map/all_to_all | solution.py:62
  1416.1 20.9 %copy-start.1 = (bf16[400,400]{1,0:T(8,128)(2,1)S(1)}, bf16[400,400]{1,0:T(8,128)(2,1)}, u32[]{:S(2)}) copy-start(bf16[400,400]{1,0:T(8,128)(2,1)} %param.6) | copy-start | bytes 960004
where the time goes:
time: 1450 us; the launch traced here: 1440 us
  waiting for transfers between devices  653 us (45%)
  blocking collectives  326 us (22%)
  local copies, waits for them, and re-layouts  324 us (22%)
  matrix products  86.6 us (6%)
  other arithmetic  28.3 us (2%)
  starting transfers between devices  14.8 us (1%)
    all_to_all x1, waiting for transfers between devices, local(): lax.all_to_all(product, ('act', 'virt'), split_axis=0, concat_axis=1, til...  327 us
    all_to_all x1, waiting for transfers between devices, local(): lax.all_to_all(halved_rows, ('act', 'virt'), split_axis=1, concat_axis=0,...  327 us
    psum x1, blocking collectives, local(): squares_total = lax.psum(jnp.sum(resid * resid), ('act', 'virt'))  167 us
    convert_element_type x5, local copies, waits for them, and re-layouts, local(): sigma_rows = left_portion.astype(jnp.float32) + right_part + active_rows  132 us
    all_to_all x1, blocking collectives, local(): lax.all_to_all(amplitudes, 'act', split_axis=1, concat_axis=0, tiled=True)  122 us
    reshape x2, local copies, waits for them, and re-layouts, local(): halved_rows.reshape(shape_abt)  38.1 us
    psum x1, blocking collectives, local(): lax.psum((numer_local, denom_local), ('act', 'virt'))  37.3 us
    dot_general x1, matrix products, local(): jnp.einsum('cb,act->abt', virtual_fock_block, halved_rows, preferred_elem...  35.7 us
  transfers between devices with their start and end apart: 3, of which 2 were waited for; matrix products, arithmetic and copies ran while one was open for 2% of the time, Pallas kernels for 0%

commit v1 on v0

v1 whole, which is shorter than its diff:
```python
import functools

import jax
import jax.numpy as jnp
from jax import lax
from jax.experimental import pallas as pl
from jax.experimental.pallas import tpu as pltpu
from jax.sharding import PartitionSpec as P

MESH = pl.DeviceIdType.MESH
AHEAD = 4


def left_kernel(peers, pair_count, fock_ref, image_ref, out_ref, held, made, sent, landed, back_sent, back_landed):
    group = lax.axis_index("act")
    me = lax.axis_index("virt")
    rounds = held.shape[0]
    barrier = pltpu.get_barrier_semaphore()
    for peer in range(peers):

        @pl.when(peer != me)
        def _():
            pl.semaphore_signal(barrier, inc=1, device_id=(group, peer), device_id_type=MESH)

    pl.semaphore_wait(barrier, peers - 1)

    def forward(r, peer):
        return pltpu.make_async_remote_copy(
            src_ref=image_ref.at[r * peers + peer], dst_ref=held.at[r, me],
            send_sem=sent.at[r, peer], recv_sem=landed.at[r, me],
            device_id=(group, peer), device_id_type=MESH)

    def forward_own(r):
        return pltpu.make_async_copy(image_ref.at[r * peers + me], held.at[r, me], landed.at[r, me])

    def backward(r, peer):
        return pltpu.make_async_remote_copy(
            src_ref=made.at[r, peer], dst_ref=out_ref.at[r * peers + me],
            send_sem=back_sent.at[r, peer], recv_sem=back_landed.at[r, me],
            device_id=(group, peer), device_id_type=MESH)

    def backward_own(r):
        return pltpu.make_async_copy(made.at[r, me], out_ref.at[r * peers + me], back_landed.at[r, me])

    def arrival(r, peer):
        return pltpu.make_async_remote_copy(
            src_ref=made.at[r, peer], dst_ref=held.at[r, peer],
            send_sem=sent.at[r, peer], recv_sem=landed.at[r, peer],
            device_id=(group, peer), device_id_type=MESH)

    def back_arrival(r, peer):
        return pltpu.make_async_remote_copy(
            src_ref=made.at[r, peer], dst_ref=out_ref.at[r * peers + peer],
            send_sem=back_sent.at[r, peer], recv_sem=back_landed.at[r, peer],
            device_id=(group, peer), device_id_type=MESH)

    def launch(r):
        for step in range(peers):
            peer = lax.rem(me + step, peers)

            @pl.when(r * peers + peer < pair_count)
            def _(step=step, peer=peer):
                if step == 0:
                    forward_own(r).start()
                else:
                    forward(r, peer).start()

    for r in range(min(AHEAD, rounds)):
        launch(r)

    def body(r, carry):
        @pl.when(r + AHEAD < rounds)
        def _():
            launch(r + AHEAD)

        @pl.when(r * peers + me < pair_count)
        def _():
            forward_own(r).wait()
            for step in range(1, peers):
                arrival(r, lax.rem(me + step, peers)).wait_recv()
            rows, width = held.shape[2], held.shape[3]
            block = held[r].reshape(peers * rows, width)
            product = jnp.dot(fock_ref[...], block, preferred_element_type=jnp.float32)
            made[r] = product.astype(jnp.bfloat16).reshape(peers, rows, width)
            backward_own(r).start()
            for step in range(1, peers):
                backward(r, lax.rem(me + step, peers)).start()

        return carry

    lax.fori_loop(0, rounds, body, 0)

    def drain(r, carry):
        mine = r * peers + me < pair_count

        @pl.when(mine)
        def _():
            backward_own(r).wait()

        for step in range(1, peers):
            peer = lax.rem(me + step, peers)

            @pl.when(r * peers + peer < pair_count)
            def _(peer=peer):
                forward(r, peer).wait_send()
                back_arrival(r, peer).wait_recv()

            @pl.when(mine)
            def _(peer=peer):
                backward(r, peer).wait_send()

        return carry

    lax.fori_loop(0, rounds, drain, 0)


def apply_left(image, fock, peers):
    pairs, rows, width = image.shape
    padded = -(-rows // 16) * 16
    if padded != rows:
        image = jnp.pad(image, ((0, 0), (0, padded - rows), (0, 0)))
        spread = jnp.pad(
            fock.reshape(peers, rows, peers, rows),
            ((0, 0), (0, padded - rows), (0, 0), (0, padded - rows)))
        fock = spread.reshape(peers * padded, peers * padded)
    rounds = -(-pairs // peers)
    out = pl.pallas_call(
        functools.partial(left_kernel, peers, pairs),
        out_shape=jax.ShapeDtypeStruct(image.shape, jnp.bfloat16),
        in_specs=[pl.BlockSpec(memory_space=pltpu.VMEM), pl.BlockSpec(memory_space=pl.ANY)],
        out_specs=pl.BlockSpec(memory_space=pl.ANY),
        scratch_shapes=[
            pltpu.VMEM((rounds, peers, padded, width), jnp.bfloat16),
            pltpu.VMEM((rounds, peers, padded, width), jnp.bfloat16),
            pltpu.SemaphoreType.DMA((rounds, peers)),
            pltpu.SemaphoreType.DMA((rounds, peers)),
            pltpu.SemaphoreType.DMA((rounds, peers)),
            pltpu.SemaphoreType.DMA((rounds, peers)),
        ],
        compiler_params=pltpu.CompilerParams(
            collective_id=0, has_side_effects=True, vmem_limit_bytes=48 * 2**20),
        cost_estimate=pl.CostEstimate(
            flops=2 * pairs * rows * rows * peers * width, bytes_accessed=800 * 2**20, transcendentals=0),
    )(fock, image)
    return out[:, :rows, :]


def local(amplitudes, virtual_fock_block, metric, active_block):
    pairs, rows, width = amplitudes.shape
    peers = lax.axis_size("virt")
    trial = lax.all_to_all(amplitudes, "act", split_axis=1, concat_axis=0, tiled=True)
    flat = trial.reshape(trial.shape[0], -1)
    weighted_flat = jnp.dot(metric, flat, preferred_element_type=jnp.float32).astype(jnp.bfloat16)
    active_flat = jnp.dot(active_block, flat, preferred_element_type=jnp.float32).astype(jnp.bfloat16)
    weighted = lax.all_to_all(weighted_flat.reshape(trial.shape), "act", split_axis=0, concat_axis=1, tiled=True)
    active = lax.all_to_all(active_flat.reshape(trial.shape), "act", split_axis=0, concat_axis=1, tiled=True)
    left = apply_left(weighted, virtual_fock_block, peers)
    right = jnp.einsum("tac,cb->tab", weighted, virtual_fock_block, preferred_element_type=jnp.float32)
    sigma = left.astype(jnp.float32) + right + active.astype(jnp.float32)
    wide = amplitudes.astype(jnp.float32)
    numer_local = jnp.sum(wide * sigma)
    denom_local = jnp.sum(wide * weighted.astype(jnp.float32))
    numerator, denominator = lax.psum((numer_local, denom_local), ("act", "virt"))
    rayleigh = numerator / denominator
    resid = sigma - rayleigh * weighted.astype(jnp.float32)
    squares = lax.psum(jnp.sum(resid * resid), ("act", "virt"))
    return resid.astype(jnp.bfloat16), rayleigh, squares / denominator


def solution(mesh):
    placed = (P("act", "virt", None), P(), P(), P())
    return jax.shard_map(
        local,
        mesh=mesh,
        in_specs=placed,
        out_specs=(P("act", "virt", None), P(), P()),
        check_vma=False,
    )
```

time: 1450 us -> 1090 us (0.75)
  Pallas kernels: 0 us -> 442 us
  waiting for transfers between devices: 653 us -> 227 us
  local copies, waits for them, and re-layouts: 324 us -> 108 us
  blocking collectives: 326 us -> 207 us
  matrix products: 86.6 us -> 56.3 us
    pallas_call x0 -> x1, Pallas kernels: none -> 442 us  [apply_left(): pl.pallas_call(functools.partial(left_kernel, peers, pairs), out_shape=ja...]
    all_to_all x3 -> x2, waiting for transfers between devices: 653 us -> 227 us  [the longest x1 122 us: local(): lax.all_to_all(active_flat.reshape(trial.shape), 'act', split_axis=0, con...]
    psum x1, blocking collectives: 167 us -> 40.2 us  [local(): squares = lax.psum(jnp.sum(resid * resid), ('act', 'virt'))]
    convert_element_type x6 -> x2, local copies, waits for them, and re-layouts: 146 us -> 35.3 us  [local(): sigma = left.astype(jnp.float32) + right + active.astype(jnp.float32)]
    reshape x6 -> x2, local copies, waits for them, and re-layouts: 83.2 us -> 32.7 us  [the longest x1 16.3 us: local(): active_flat.reshape(trial.shape)]
    dot_general x4 -> x3, matrix products: 86.6 us -> 56.3 us  [the longest x1 36.3 us: local(): jnp.einsum('tac,cb->tab', weighted, virtual_fock_block, preferred_element...]
    all_to_all x3 -> x2, local copies, waits for them, and re-layouts: 46.7 us -> 20.9 us  [local(): lax.all_to_all(weighted_flat.reshape(trial.shape), 'act', split_axis=0, c...]
    mul x1 -> x0, other arithmetic: 17.7 us -> none  [local(): resid = sigma_rows - rayleigh * weighted_rows]
  transfers between devices with their start and end apart: 3 -> 2, of which waited for: 2 -> 2; matrix products, arithmetic and copies ran while one was open for 2% -> 4% of each run, Pallas kernels for 0% -> 0%
where the time goes in v1:
time: 1090 us
  Pallas kernels  442 us (41%)
  waiting for transfers between devices  227 us (21%)
  blocking collectives  207 us (19%)
  local copies, waits for them, and re-layouts  108 us (10%)
  matrix products  56.3 us (5%)
  other arithmetic  29.2 us (3%)
  starting transfers between devices  12.7 us (1%)
    pallas_call x1, Pallas kernels, apply_left(): pl.pallas_call(functools.partial(left_kernel, peers, pairs), out_shape=ja...  442 us
    all_to_all x1, blocking collectives, local(): lax.all_to_all(amplitudes, 'act', split_axis=1, concat_axis=0, tiled=True)  122 us
    all_to_all x1, waiting for transfers between devices, local(): lax.all_to_all(active_flat.reshape(trial.shape), 'act', split_axis=0, con...  122 us
    all_to_all x1, waiting for transfers between devices, local(): lax.all_to_all(weighted_flat.reshape(trial.shape), 'act', split_axis=0, c...  105 us
    psum x1, blocking collectives, local(): lax.psum((numer_local, denom_local), ('act', 'virt'))  44.3 us
    psum x1, blocking collectives, local(): squares = lax.psum(jnp.sum(resid * resid), ('act', 'virt'))  40.2 us
    dot_general x1, matrix products, local(): jnp.einsum('tac,cb->tab', weighted, virtual_fock_block, preferred_element...  36.3 us
    convert_element_type x2, local copies, waits for them, and re-layouts, local(): sigma = left.astype(jnp.float32) + right + active.astype(jnp.float32)  35.3 us
  transfers between devices with their start and end apart: 2, of which 2 were waited for; matrix products, arithmetic and copies ran while one was open for 4% of the time, Pallas kernels for 0%

profile of v1, /device:TPU:0, one launch (start us, length us, event | category | flops | bytes accessed | tf_op | source)
XLA Modules:
  0.0 1088.4 jit_solution(17764331804311536142)
XLA Ops:
  0.6 0.0 copy-start
  0.6 7.3 copy.27
  7.9 122.3 %all_to_all.42 = bf16[100,80,640]{2,0,1:T(8,128)(2,1)S(1)} all-to-all(bf16[100,80,640]{2,0,1:T(8,128)(2,1)S(1)} %copy.27), channel_id=1, replica_groups=mesh['act'=4,'virt'=8] {'act'}, dimensions={1} | all-to-all | bytes 20480000 | tf_op jit(solution)/shard_map/all_to_all | solution.py:151
  130.2 4.5 copy.28
  134.7 3.9 copy.39
  138.7 0.0 copy-start.3
  138.7 3.8 copy-done.3
  142.5 0.0 copy-done
  142.5 8.0 convolution_convert_fusion.1
  150.5 16.3 %reshape.21 = bf16[400,20,640]{2,1,0:T(8,128)(2,1)} reshape(bf16[400,12800]{1,0:T(8,128)(2,1)} %convolution_convert_fusion.1) | data formatting | bytes 20480000 | tf_op jit(solution)/shard_map/reshape | solution.py:155
  166.8 0.0 copy-start.4
  166.8 6.4 all-to-all-start.1
  173.2 0.0 copy-done.4
  173.2 11.9 %convolution_convert_fusion = bf16[400,12800]{1,0:T(8,128)(2,1)} fusion(bf16[400,400]{1,0:T(8,128)(2,1)S(1)} %copy-done.4, bf16[400,12800]{1,0:T(8,128)(2,1)} %bitcast.32), kind=kOutput, calls=%fused_computation.8 | convolution fusion | flops 4101120000 | bytes 20800000 | tf_op jit(solution)/shard_map/dot_general | solution.py:154
  185.2 16.3 %reshape.22 = bf16[400,20,640]{2,1,0:T(8,128)(2,1)} reshape(bf16[400,12800]{1,0:T(8,128)(2,1)} %convolution_convert_fusion) | data formatting | bytes 20480000 | tf_op jit(solution)/shard_map/reshape | solution.py:156
  201.5 104.9 %all-to-all-done.1 = bf16[400,20,640]{2,1,0:T(8,128)(2,1)} async-done(((bf16[400,20,640]{2,1,0:T(8,128)(2,1)}), bf16[400,20,640]{2,1,0:T(8,128)(2,1)}, u32[]{:S(2)}, u32[]{:S(2)}) %all-to-all-start.1) | async-done | bytes 10240032 | tf_op jit(solution)/shard_map/all_to_all | solution.py:155
  306.4 6.3 all-to-all-start.2
  312.7 11.5 %copy.30 = bf16[100,4,20,640]{3,0,2,1:T(8,128)(2,1)} copy(bf16[100,4,20,640]{3,2,0,1:T(8,128)(2,1)} %bitcast.4) | data formatting | bytes 20480000 | tf_op jit(solution)/shard_map/all_to_all | solution.py:155
  324.2 122.2 %all-to-all-done.2 = bf16[400,20,640]{2,1,0:T(8,128)(2,1)} async-done(((bf16[400,20,640]{2,1,0:T(8,128)(2,1)}), bf16[400,20,640]{2,1,0:T(8,128)(2,1)}, u32[]{:S(2)}, u32[]{:S(2)}) %all-to-all-start.2) | async-done | bytes 10240032 | tf_op jit(solution)/shard_map/all_to_all | solution.py:156
  446.4 12.3 %copy_convert_fusion = f32[400,20,640]{2,0,1:T(8,128)} fusion(bf16[400,20,640]{2,1,0:T(8,128)(2,1)} %all-to-all-done.2), kind=kLoop, calls=%fused_computation.11 | loop fusion | flops 5120000 | bytes 30720000 | tf_op jit(solution)/shard_map/convert_element_type | solution.py:159
  458.7 19.6 %reshape.24 = f32[4,100,20,640]{3,1,0,2:T(8,128)} reshape(f32[400,20,640]{2,0,1:T(8,128)} %copy_convert_fusion) | data formatting | bytes 40960000 | tf_op jit(solution)/shard_map/convert_element_type | solution.py:159
  478.3 15.7 %copy.34 = f32[100,4,20,640]{3,0,2,1:T(8,128)} copy(f32[100,4,20,640]{3,0,1,2:T(8,128)} %bitcast.28) | data formatting | bytes 40960000 | tf_op jit(solution)/shard_map/convert_element_type | solution.py:159
  494.0 0.0 copy-start.2
  494.0 9.4 copy.31.image_ref
  503.4 0.0 copy-done.2
  503.4 442.3 %shard_map.67 = bf16[100,80,640]{2,1,0:T(8,128)(2,1)} custom-call(bf16[640,640]{1,0:T(8,128)(2,1)S(1)} %copy-done.2, bf16[100,80,640]{2,1,0:T(8,128)(2,1)} %copy.31.image_ref), custom_call_target="tpu_custom_call" | custom-call | flops 6553600000 | bytes 838860800 | tf_op jit(solution)/shard_map/pallas_call | solution.py:127
  945.7 36.3 %fusion.1 = (f32[]{:T(128)}, f32[]{:T(128)}, f32[100,80,640]{2,1,0:T(8,128)}) fusion(bf16[100,80,640]{2,1,0:T(8,128)(2,1)} %copy.31.image_ref, bf16[100,80,640]{2,1,0:T(8,128)(2,1)} %param.4, f32[100,80,640]{2,0,1:T(8,128)} %bitcast.25, bf16[640,640]{1,0:T(8,128)(2,1)S(1)} %copy-done.2, bf16[100,80,640]{2,1,0:T(8,128)(2,1)} %shard_map.67), kind=kOutput, calls=%fused_computation.4 | convolution fusion | flops 6599680000 | bytes 72499208 | tf_op jit(solution)/shard_map/tac,cb->tab/dot_general | solution.py:158
  982.1 44.3 %all-reduce = (f32[]{:T(128)}, f32[]{:T(128)}) all-reduce(f32[]{:T(128)} %get-tuple-element.4, f32[]{:T(128)} %get-tuple-element.3), channel_id=1, replica_groups=mesh['act'=4,'virt'=8] {'act','virt'}, use_global_device_ids=true, to_apply=%region_1.0 | all-reduce | flops 2 | bytes 16 | tf_op jit(solution)/shard_map/psum | solution.py:163
  1027.7 0.0 copy-start.1
  1027.7 16.9 %multiply_reduce_fusion = (f32[]{:T(128)}, bf16[100,80,640]{2,1,0:T(8,128)(2,1)}) fusion(f32[100,80,640]{2,1,0:T(8,128)} %get-tuple-element.9, f32[]{:T(128)} %div.6, bf16[100,80,640]{2,0,1:T(8,128)(2,1)} %bitcast.27), kind=kLoop, calls=%fused_computation.7 | loop fusion | flops 30720000 | bytes 40960008 | tf_op jit(solution)/shard_map/reduce_sum | solution.py:166
  1044.6 40.2 %psum.23 = f32[]{:T(128)} all-reduce(f32[]{:T(128)} %get-tuple-element.7), channel_id=1, replica_groups=mesh['act'=4,'virt'=8] {'act','virt'}, use_global_device_ids=true, to_apply=%region_5.0 | all-reduce | flops 1 | bytes 8 | tf_op jit(solution)/shard_map/psum | solution.py:166
  1086.2 0.0 copy-done.1
Async XLA Ops:
  0.6 141.9 %copy-start = (bf16[400,400]{1,0:T(8,128)(2,1)S(1)}, bf16[400,400]{1,0:T(8,128)(2,1)}, u32[]{:S(2)}) copy-start(bf16[400,400]{1,0:T(8,128)(2,1)} %param.6) | copy-start | bytes 960004
  138.7 3.8 copy-start.3
  166.8 6.4 copy-start.4
  166.8 139.6 %all-to-all-start.1 = ((bf16[400,20,640]{2,1,0:T(8,128)(2,1)}), bf16[400,20,640]{2,1,0:T(8,128)(2,1)}, u32[]{:S(2)}, u32[]{:S(2)}) async-start(bf16[400,20,640]{2,1,0:T(8,128)(2,1)} %reshape.21), calls=%async_computation.1 | async-start | bytes 24576000 | tf_op jit(solution)/shard_map/all_to_all | solution.py:155
  306.4 139.9 %all-to-all-start.2 = ((bf16[400,20,640]{2,1,0:T(8,128)(2,1)}), bf16[400,20,640]{2,1,0:T(8,128)(2,1)}, u32[]{:S(2)}, u32[]{:S(2)}) async-start(bf16[400,20,640]{2,1,0:T(8,128)(2,1)} %reshape.22), calls=%async_computation.2 | async-start | bytes 24576000 | tf_op jit(solution)/shard_map/all_to_all | solution.py:156
  494.0 9.4 copy-start.2
  1027.7 58.5 %copy-start.1 = (bf16[400,400]{1,0:T(8,128)(2,1)S(1)}, bf16[400,400]{1,0:T(8,128)(2,1)}, u32[]{:S(2)}) copy-start(bf16[400,400]{1,0:T(8,128)(2,1)} %param.6) | copy-start | bytes 960004

commit v2 on v1

v2 whole, which is shorter than its diff:
```python
import functools

import jax
import jax.numpy as jnp
from jax import lax
from jax.experimental import pallas as pl
from jax.experimental.pallas import tpu as pltpu
from jax.sharding import PartitionSpec as P

MESH = pl.DeviceIdType.MESH
AHEAD = 4


def stage_kernel(first, peers, groups, pair_count, start, *refs):
    if first:
        (shift_ref, fock_ref, metric_ref, active_ref, image_ref, rows_ref,
         left_ref, back_ref, kept_ref) = refs[:9]
        scratch = refs[9:]
    else:
        fock_ref, metric_ref, kept_ref, image_ref, rows_ref, left_ref, back_ref = refs[:7]
        scratch = refs[7:]
    (held, made, row_held, row_made, sent, landed, back_sent, back_landed,
     row_sent, row_landed, row_back_sent, row_back_landed) = scratch
    group = lax.axis_index("act")
    me = lax.axis_index("virt")
    rounds, rows, width = held.shape[0], held.shape[2], held.shape[3]
    items = row_held.shape[0]
    per_step = -(-items // rounds)
    barrier = pltpu.get_barrier_semaphore()
    for step in range(1, peers):
        pl.semaphore_signal(
            barrier, inc=1, device_id=(group, lax.rem(me + step, peers)), device_id_type=MESH)
    for step in range(1, groups):
        pl.semaphore_signal(
            barrier, inc=1, device_id=(lax.rem(group + step, groups), me), device_id_type=MESH)
    pl.semaphore_wait(barrier, peers + groups - 2)

    def slab(t):
        return image_ref.at[t, :, pl.ds(start, width)]

    def forward(r, peer):
        return pltpu.make_async_remote_copy(
            src_ref=slab(r * peers + peer), dst_ref=held.at[r, me],
            send_sem=sent.at[r, peer], recv_sem=landed.at[r, me],
            device_id=(group, peer), device_id_type=MESH)

    def forward_own(r):
        return pltpu.make_async_copy(slab(r * peers + me), held.at[r, me], landed.at[r, me])

    def arrival(r, peer):
        return pltpu.make_async_remote_copy(
            src_ref=made.at[r, peer], dst_ref=held.at[r, peer],
            send_sem=sent.at[r, peer], recv_sem=landed.at[r, peer],
            device_id=(group, peer), device_id_type=MESH)

    def backward(r, peer):
        return pltpu.make_async_remote_copy(
            src_ref=made.at[r, peer], dst_ref=left_ref.at[r * peers + me],
            send_sem=back_sent.at[r, peer], recv_sem=back_landed.at[r, me],
            device_id=(group, peer), device_id_type=MESH)

    def backward_own(r):
        return pltpu.make_async_copy(made.at[r, me], left_ref.at[r * peers + me], back_landed.at[r, me])

    def back_arrival(r, peer):
        return pltpu.make_async_remote_copy(
            src_ref=made.at[r, peer], dst_ref=left_ref.at[r * peers + peer],
            send_sem=back_sent.at[r, peer], recv_sem=back_landed.at[r, peer],
            device_id=(group, peer), device_id_type=MESH)

    def row_forward(i, peer):
        return pltpu.make_async_remote_copy(
            src_ref=rows_ref.at[peer * items + i], dst_ref=row_held.at[i, group],
            send_sem=row_sent.at[i, peer], recv_sem=row_landed.at[i, group],
            device_id=(peer, me), device_id_type=MESH)

    def row_forward_own(i):
        return pltpu.make_async_copy(
            rows_ref.at[group * items + i], row_held.at[i, group], row_landed.at[i, group])

    def row_arrival(i, peer):
        return pltpu.make_async_remote_copy(
            src_ref=rows_ref.at[peer * items + i], dst_ref=row_held.at[i, peer],
            send_sem=row_sent.at[i, peer], recv_sem=row_landed.at[i, peer],
            device_id=(peer, me), device_id_type=MESH)

    def row_backward(i, peer):
        return pltpu.make_async_remote_copy(
            src_ref=row_made.at[i, peer], dst_ref=back_ref.at[group * items + i],
            send_sem=row_back_sent.at[i, peer], recv_sem=row_back_landed.at[i, group],
            device_id=(peer, me), device_id_type=MESH)

    def row_backward_own(i):
        return pltpu.make_async_copy(
            row_made.at[i, group], back_ref.at[group * items + i], row_back_landed.at[i, group])

    def row_back_arrival(i, peer):
        return pltpu.make_async_remote_copy(
            src_ref=row_made.at[i, peer], dst_ref=back_ref.at[peer * items + i],
            send_sem=row_back_sent.at[i, peer], recv_sem=row_back_landed.at[i, peer],
            device_id=(peer, me), device_id_type=MESH)

    def launch(r):
        for step in range(peers):
            peer = lax.rem(me + step, peers)

            @pl.when(r * peers + peer < pair_count)
            def _(step=step, peer=peer):
                if step == 0:
                    forward_own(r).start()
                else:
                    forward(r, peer).start()

        def launch_row(i, carry):
            row_forward_own(i).start()
            for step in range(1, groups):
                row_forward(i, lax.rem(group + step, groups)).start()
            return carry

        lax.fori_loop(jnp.minimum(r * per_step, items), jnp.minimum((r + 1) * per_step, items), launch_row, 0)

    def ahead(r, carry):
        launch(r)
        return carry

    lax.fori_loop(0, min(AHEAD, rounds), ahead, 0)

    def mix(matrix_ref, i):
        total = jnp.dot(matrix_ref[0], row_held[i, 0], preferred_element_type=jnp.float32)
        for q in range(1, groups):
            total += jnp.dot(matrix_ref[q], row_held[i, q], preferred_element_type=jnp.float32)
        return total

    def mix_row(i, carry):
        row_forward_own(i).wait()
        for step in range(1, groups):
            row_arrival(i, lax.rem(group + step, groups)).wait_recv()
        tall = row_held.shape[2]
        weighted = mix(metric_ref, i)
        if first:
            half = weighted.astype(jnp.bfloat16)
            row_made[i] = half.reshape(groups, tall, -1)
            active = mix(active_ref, i) - shift_ref[0] * (weighted - half.astype(jnp.float32))
            kept_ref[i] = active.astype(jnp.bfloat16).reshape(groups, tall, -1)
        else:
            wide = row_held.shape[3]
            kept = kept_ref[i, :, :, :wide].astype(jnp.float32)
            row_made[i, :, :, :wide] = (kept + weighted.reshape(groups, tall, wide)).astype(jnp.bfloat16)
            row_made[i, :, :, wide:] = kept_ref[i, :, :, wide:]
        row_backward_own(i).start()
        for step in range(1, groups):
            row_backward(i, lax.rem(group + step, groups)).start()
        return carry

    def body(r, carry):
        @pl.when(r + AHEAD < rounds)
        def _():
            launch(r + AHEAD)

        lax.fori_loop(jnp.minimum(r * per_step, items), jnp.minimum((r + 1) * per_step, items), mix_row, 0)

        @pl.when(r * peers + me < pair_count)
        def _():
            forward_own(r).wait()
            for step in range(1, peers):
                arrival(r, lax.rem(me + step, peers)).wait_recv()
            block = held[r].reshape(peers * rows, width)
            product = jnp.dot(fock_ref[...], block, preferred_element_type=jnp.float32)
            made[r] = product.astype(jnp.bfloat16).reshape(peers, rows, width)
            backward_own(r).start()
            for step in range(1, peers):
                backward(r, lax.rem(me + step, peers)).start()

        return carry

    lax.fori_loop(0, rounds, body, 0)

    def drain(r, carry):
        mine = r * peers + me < pair_count

        @pl.when(mine)
        def _():
            backward_own(r).wait()

        for step in range(1, peers):
            peer = lax.rem(me + step, peers)

            @pl.when(r * peers + peer < pair_count)
            def _(peer=peer):
                forward(r, peer).wait_send()
                back_arrival(r, peer).wait_recv()

            @pl.when(mine)
            def _(peer=peer):
                backward(r, peer).wait_send()

        return carry

    lax.fori_loop(0, rounds, drain, 0)

    def drain_row(i, carry):
        row_backward_own(i).wait()
        for step in range(1, groups):
            peer = lax.rem(group + step, groups)
            row_forward(i, peer).wait_send()
            row_back_arrival(i, peer).wait_recv()
            row_backward(i, peer).wait_send()
        return carry

    lax.fori_loop(0, items, drain_row, 0)


def stage(first, peers, groups, pairs, start, width, smalls, kept, image, turned):
    fock = smalls[1] if first else smalls[0]
    padded = image.shape[1]
    count, tall, row_width = turned.shape
    items = count // groups
    rounds = -(-pairs // peers)
    full = image.shape[2]
    whole = pl.BlockSpec(memory_space=pltpu.VMEM)
    anywhere = pl.BlockSpec(memory_space=pl.ANY)
    made_rows = (items, groups, tall, full)
    out_shape = [
        jax.ShapeDtypeStruct((pairs, padded, width), jnp.bfloat16),
        jax.ShapeDtypeStruct((count, tall, full), jnp.bfloat16),
    ]
    out_specs = [anywhere, anywhere]
    if first:
        in_specs = [pl.BlockSpec(memory_space=pltpu.SMEM)] + [whole] * 3
        out_shape.append(jax.ShapeDtypeStruct(made_rows, jnp.bfloat16))
        out_specs.append(whole)
        operands = smalls
    else:
        in_specs = [whole] * 3
        operands = (*smalls, kept)
    dma = pltpu.SemaphoreType.DMA
    return pl.pallas_call(
        functools.partial(stage_kernel, first, peers, groups, pairs, start),
        out_shape=out_shape,
        in_specs=in_specs + [anywhere] * 2,
        out_specs=out_specs,
        scratch_shapes=[
            pltpu.VMEM((rounds, peers, padded, width), jnp.bfloat16),
            pltpu.VMEM((rounds, peers, padded, width), jnp.bfloat16),
            pltpu.VMEM((items, groups, tall, row_width), jnp.bfloat16),
            pltpu.VMEM(made_rows, jnp.bfloat16),
            dma((rounds, peers)), dma((rounds, peers)), dma((rounds, peers)), dma((rounds, peers)),
            dma((items, groups)), dma((items, groups)), dma((items, groups)), dma((items, groups)),
        ],
        compiler_params=pltpu.CompilerParams(
            collective_id=1 if first else 2, has_side_effects=True, vmem_limit_bytes=60 * 2**20),
        cost_estimate=pl.CostEstimate(
            flops=2 * pairs * fock.size * width, bytes_accessed=400 * 2**20, transcendentals=0),
    )(*operands, image, turned)


def sum_kernel(groups, peers, part_ref, total_ref, slots, sent, landed):
    group, me = lax.axis_index("act"), lax.axis_index("virt")
    count = groups * peers
    mine = group * peers + me
    barrier = pltpu.get_barrier_semaphore()

    def target(step):
        other = lax.rem(mine + step, count)
        return other, (other // peers, lax.rem(other, peers))

    def greet(step, carry):
        pl.semaphore_signal(barrier, inc=1, device_id=target(step)[1], device_id_type=MESH)
        return carry

    lax.fori_loop(1, count, greet, 0)
    pl.semaphore_wait(barrier, count - 1)

    def copy(step, slot):
        other, place = target(step)
        return pltpu.make_async_remote_copy(
            src_ref=part_ref, dst_ref=slots.at[slot], send_sem=sent.at[other], recv_sem=landed.at[slot],
            device_id=place, device_id_type=MESH)

    def send(step, carry):
        copy(step, mine).start()
        return carry

    lax.fori_loop(1, count, send, 0)
    slots[mine] = part_ref[...]

    def receive(step, carry):
        copy(step, target(step)[0]).wait_recv()
        return carry

    lax.fori_loop(1, count, receive, 0)
    total_ref[...] = jnp.sum(slots[...], axis=0)

    def finish(step, carry):
        copy(step, mine).wait_send()
        return carry

    lax.fori_loop(1, count, finish, 0)


def sum_all(values, groups, peers, number):
    part = jnp.zeros((8, 128), jnp.float32)
    for at, value in enumerate(values):
        part = part.at[at].set(value)
    total = pl.pallas_call(
        functools.partial(sum_kernel, groups, peers),
        out_shape=jax.ShapeDtypeStruct(part.shape, jnp.float32),
        in_specs=[pl.BlockSpec(memory_space=pltpu.VMEM)],
        out_specs=pl.BlockSpec(memory_space=pltpu.VMEM),
        scratch_shapes=[
            pltpu.VMEM((groups * peers, *part.shape), jnp.float32),
            pltpu.SemaphoreType.DMA((groups * peers,)),
            pltpu.SemaphoreType.DMA((groups * peers,)),
        ],
        compiler_params=pltpu.CompilerParams(collective_id=number, has_side_effects=True),
    )(part)
    return [total[at, 0] for at in range(len(values))]


def local(amplitudes, virtual_fock_block, metric, active_block):
    pairs, rows, width = amplitudes.shape
    peers, groups = lax.axis_size("virt"), lax.axis_size("act")
    fock = virtual_fock_block
    padded = -(-rows // 16) * 16
    tall = -(-pairs // 8) * 8
    cut = (3 * width // 5) // 128 * 128

    def widen(array):
        if padded == rows:
            return array
        return jnp.pad(array, ((0, 0), (0, padded - rows), (0, 0)))

    def turn(array):
        return jnp.pad(jnp.transpose(array, (1, 0, 2)), ((0, 0), (0, tall - pairs), (0, 0)))

    def turn_back(array):
        return jnp.transpose(array, (1, 0, 2))[:pairs]

    def pair_matrix(array):
        room = tall - pairs
        spread = jnp.pad(
            array.reshape(groups, pairs, groups, pairs), ((0, 0), (0, room), (0, 0), (0, room)))
        return jnp.transpose(spread, (2, 0, 1, 3)).reshape(groups, groups * tall, tall)

    spread = fock
    if padded != rows:
        room = padded - rows
        spread = jnp.pad(
            fock.reshape(peers, rows, peers, rows), ((0, 0), (0, room), (0, 0), (0, room))
        ).reshape(peers * padded, peers * padded)
    metric_parts, active_parts = pair_matrix(metric), pair_matrix(active_block)
    shift = (2.0 / fock.shape[0]) * jnp.sum(jnp.diagonal(fock).astype(jnp.float32))
    applied, weighted_turned, kept = stage(
        True, peers, groups, pairs, 0, cut, (shift.reshape(1), spread, metric_parts, active_parts),
        None, widen(amplitudes), turn(amplitudes))
    weighted = turn_back(weighted_turned)
    left, rest_turned = stage(
        False, peers, groups, pairs, cut, width - cut, (spread, metric_parts),
        kept, widen(weighted), turn(applied[:, :rows]))
    rest = turn_back(rest_turned)
    right = jnp.einsum("tac,cb->tab", weighted, fock, preferred_element_type=jnp.float32)
    left_wide = jnp.pad(left[:, :rows], ((0, 0), (0, 0), (cut, 0)))
    sigma = left_wide.astype(jnp.float32) + right + rest.astype(jnp.float32)
    wide = amplitudes.astype(jnp.float32)
    weighted_wide = weighted.astype(jnp.float32)
    numer_local = jnp.sum(wide * sigma)
    denom_local = jnp.sum(wide * weighted_wide)
    numerator, denominator = sum_all((numer_local, denom_local), groups, peers, 3)
    rayleigh = numerator / denominator
    resid = sigma - rayleigh * weighted_wide
    squares, = sum_all((jnp.sum(resid * resid),), groups, peers, 4)
    return resid.astype(jnp.bfloat16), rayleigh, squares / denominator


def solution(mesh):
    placed = (P("act", "virt", None), P(), P(), P())
    return jax.shard_map(
        local,
        mesh=mesh,
        in_specs=placed,
        out_specs=(P("act", "virt", None), P(), P()),
        check_vma=False,
    )
```

time: 1090 us -> 623 us (0.57)
  waiting for transfers between devices: 227 us -> 0 us
  blocking collectives: 207 us -> 0 us
  Pallas kernels: 442 us -> 503 us
  local copies, waits for them, and re-layouts: 108 us -> 64.4 us
  matrix products: 56.3 us -> 30.6 us
  starting transfers between devices: 12.7 us -> 0 us
  other arithmetic: 29.2 us -> 17.2 us
    all_to_all x2 -> x0, waiting for transfers between devices: 227 us -> none  [the longest x1 122 us: local(): lax.all_to_all(active_flat.reshape(trial.shape), 'act', split_axis=0, con...]
    all_to_all x1 -> x0, blocking collectives: 122 us -> none  [local(): lax.all_to_all(amplitudes, 'act', split_axis=1, concat_axis=0, tiled=True)]
    psum x2 -> x0, blocking collectives: 84.4 us -> none  [the longest x1 44.3 us: local(): lax.psum((numer_local, denom_local), ('act', 'virt'))]
    pallas_call x1 -> x4, Pallas kernels: 442 us -> 503 us  [the longest x2 482 us: stage(): pl.pallas_call(functools.partial(stage_kernel, first, peers, groups, pair...]
    convert_element_type x2 -> x0, local copies, waits for them, and re-layouts: 35.3 us -> none  [local(): sigma = left.astype(jnp.float32) + right + active.astype(jnp.float32)]
    reshape x2 -> x4, local copies, waits for them, and re-layouts: 32.7 us -> 2.67 us  [pair_matrix(): array.reshape(groups, pairs, groups, pairs)]
    dot_general x3 -> x1, matrix products: 56.3 us -> 30.6 us  [local(): jnp.einsum('tac,cb->tab', weighted, fock, preferred_element_type=jnp.floa...]
    all_to_all x3 -> x0, local copies, waits for them, and re-layouts: 25.4 us -> none  [the longest x2 20.9 us: local(): lax.all_to_all(weighted_flat.reshape(trial.shape), 'act', split_axis=0, c...]
  transfers between devices with their start and end apart: 2 -> 0, of which waited for: 2 -> 0; matrix products, arithmetic and copies ran while one was open for 4% -> 0% of each run, Pallas kernels for 0% -> 0%
where the time goes in v2:
time: 623 us; the launch traced here: 622 us
  Pallas kernels  503 us (81%)
  local copies, waits for them, and re-layouts  64.4 us (10%)
  matrix products  30.6 us (5%)
  other arithmetic  17.2 us (3%)
  between operations  6.28 us (1%)
    pallas_call x2, Pallas kernels, stage(): pl.pallas_call(functools.partial(stage_kernel, first, peers, groups, pair...  482 us
    dot_general x1, matrix products, local(): jnp.einsum('tac,cb->tab', weighted, fock, preferred_element_type=jnp.floa...  30.6 us
    pallas_call x2, Pallas kernels, sum_all(): pl.pallas_call(functools.partial(sum_kernel, groups, peers), out_shape=ja...  20.9 us
    pallas_call x3, local copies, waits for them, and re-layouts, stage(): pl.pallas_call(functools.partial(stage_kernel, first, peers, groups, pair...  20.6 us
    reduce_sum x1, other arithmetic, local(): squares, = sum_all((jnp.sum(resid * resid),), groups, peers, 4)  16.5 us

profile of v2, /device:TPU:0, one launch (start us, length us, event | category | flops | bytes accessed | tf_op | source)
XLA Modules:
  0.0 621.7 jit_solution(3475378665559077515)
XLA Ops:
  0.7 9.8 %gather_fusion = bf16[640]{0:T(1024)(128)(2,1)S(1)} fusion(bf16[640,640]{1,0:T(8,128)(2,1)} %refs_0_.1, s32[640]{0:T(1024)S(1)} %or_reduce_fusion), kind=kCustom, calls=%fused_computation | custom fusion | bytes 7680 | tf_op jit(solution)/shard_map/jit(diagonal)/cond/branch_0_fun/gather | solution.py:352
  10.4 0.6 convert_reduce_fusion
  11.7 1.3 reshape.90
  13.0 0.1 copy.13
  13.0 0.9 pad.27
  13.9 1.3 reshape.93
  15.2 0.1 copy.14
  15.3 0.8 pad.28
  16.1 7.2 %copy.28 = bf16[100,80,640]{2,0,1:T(8,128)(2,1)S(1)} copy(bf16[100,80,640]{2,1,0:T(8,128)(2,1)} %refs_4_.1) | data formatting | bytes 20480000 | tf_op args[0]
  23.3 4.6 pad.29.refs_5_
  27.9 280.4 %shard_map.67 = (bf16[100,80,384]{2,1,0:T(8,128)(2,1)}, bf16[80,104,640]{2,1,0:T(8,128)(2,1)}, bf16[20,4,104,640]{3,2,1,0:T(8,128)(2,1)}) custom-call(f32[1]{0:T(128)} %bitcast.2.refs_0_, bf16[640,640]{1,0:T(8,128)(2,1)} %refs_0_.1, bf16[4,416,104]{2,1,0:T(8,128)(2,1)} %bitcast.39, bf16[4,416,104]{2,1,0:T(8,128)(2,1)} %bitcast.41, ...), custom_call_target="tpu_custom_call" | custom-call | flops 31457280000 | bytes 419430400 | tf_op jit(solution)/shard_map/pallas_call | solution.py:237
  308.3 0.0 slice-start
  308.3 4.3 copy.29
  312.6 0.0 slice-start.2
  312.6 3.3 pad.30.refs_4_
  315.9 5.0 copy.27
  320.9 8.8 %slice.64.refs_3_ = bf16[100,80,640]{2,1,0:T(8,128)(2,1)} slice(bf16[104,80,640]{2,1,0:T(8,128)(2,1)} %bitcast.31), slice={[0:100], [0:80], [0:640]} | slice | bytes 20480000 | tf_op jit(solution)/shard_map/slice | solution.py:337
  329.7 202.0 %shard_map.68 = (bf16[100,80,256]{2,1,0:T(8,128)(2,1)}, bf16[80,104,640]{2,1,0:T(8,128)(2,1)}) custom-call(bf16[640,640]{1,0:T(8,128)(2,1)} %refs_0_.1, bf16[4,416,104]{2,1,0:T(8,128)(2,1)} %bitcast.40, bf16[20,4,104,640]{3,2,1,0:T(8,128)(2,1)} %get-tuple-element.44.refs_2_, bf16[100,80,640]{2,1,0:T(8,128)(2,1)} %slice.64.refs_3_, ...), custom_call_target="tpu_custom_call" | custom-call | flops 20971520000 | bytes 419430400 | tf_op jit(solution)/shard_map/pallas_call | solution.py:237
  531.7 0.0 copy-start
  531.7 11.3 %copy.26 = bf16[80,104,640]{2,0,1:T(8,128)(2,1)} copy(bf16[80,104,640]{2,1,0:T(8,128)(2,1)} %get-tuple-element.48) | data formatting | bytes 21299200 | tf_op jit(solution)/shard_map/pallas_call | solution.py:237
  543.0 30.6 %fusion.1 = (f32[]{:T(128)}, f32[]{:T(128)}, f32[100,80,640]{2,1,0:T(8,128)}) fusion(bf16[100,80,640]{2,1,0:T(8,128)(2,1)} %refs_4_.1, bf16[104,80,640]{2,1,0:T(8,128)(2,1)} %bitcast.32, bf16[104,80,640]{2,1,0:T(8,128)(2,1)} %bitcast.38, bf16[640,640]{1,0:T(8,128)(2,1)S(1)} %copy-done, bf16[80,104,640]{2,1,0:T(8,128)(2,1)} %get-tuple-element.45, ...), kind=kOutput, calls=%fused_computation.5 | convolution fusion | flops 6604800000 | bytes 66764808 | tf_op jit(solution)/shard_map/tac,cb->tab/dot_general | solution.py:361
  573.6 0.6 broadcast.87
  574.3 0.7 scatter.19
  575.0 0.1 scatter.20
  575.1 0.6 copy-done.1
  575.6 10.9 %shard_map.69 = f32[8,128]{1,0:T(8,128)} custom-call(f32[8,128]{1,0:T(8,128)} %copy-done.1), custom_call_target="tpu_custom_call" | custom-call | tf_op jit(solution)/shard_map/pallas_call | solution.py:305
  586.5 1.3 fusion.5
  589.1 16.5 %multiply_reduce_fusion = (f32[]{:T(128)}, bf16[100,80,640]{2,1,0:T(8,128)(2,1)}) fusion(f32[100,80,640]{2,1,0:T(8,128)} %get-tuple-element.55, f32[]{:T(128)} %bitcast.12, bf16[104,80,640]{2,1,0:T(8,128)(2,1)} %bitcast.33), kind=kLoop, calls=%fused_computation.7 | loop fusion | flops 30720000 | bytes 40960008 | tf_op jit(solution)/shard_map/reduce_sum | solution.py:371
  605.7 0.6 scatter.22
  606.3 0.7 scatter.23.part_ref
  607.0 10.0 %shard_map.70 = f32[8,128]{1,0:T(8,128)} custom-call(f32[8,128]{1,0:T(8,128)} %scatter.23.part_ref), custom_call_target="tpu_custom_call" | custom-call | tf_op jit(solution)/shard_map/pallas_call | solution.py:305
  617.0 1.2 slice.61
  (9 shorter events, 0.1 us)
Async XLA Ops:
  308.3 7.6 %slice-start = ((s8[10649600]{0:T(1024)(128)(4,1)}), s8[4194304]{0:T(1024)(128)(4,1)S(1)}, s32[]{:S(2)}) async-start(s8[10649600]{0:T(1024)(128)(4,1)} %bitcast.36), calls=%async_computation | async-start | bytes 8388608
  308.3 7.6 %slice-start.1 = ((s8[10649600]{0:T(1024)(128)(4,1)}), s8[4194304]{0:T(1024)(128)(4,1)S(1)}, s32[]{:S(2)}) async-start(s8[10649600]{0:T(1024)(128)(4,1)} %bitcast.36), calls=%async_computation.1 | async-start | bytes 8388608
  312.6 3.3 slice-start.2
  531.7 11.4 %copy-start = (bf16[640,640]{1,0:T(8,128)(2,1)S(1)}, bf16[640,640]{1,0:T(8,128)(2,1)}, u32[]{:S(2)}) copy-start(bf16[640,640]{1,0:T(8,128)(2,1)} %refs_0_.1) | copy-start | bytes 2457604
  575.1 0.6 copy-start.1

commit v3 on v2

--- a/solution.py
+++ b/solution.py
@@ -254,11 +254,31 @@
     )(*operands, image, turned)
 
 
-def sum_kernel(groups, peers, part_ref, total_ref, slots, sent, landed):
+def finish_kernel(groups, peers, fock_ref, trial_ref, image_ref, left_ref, rest_ref, out_ref, stats_ref,
+                  trial, image, left, rest, sigma, part, slots, loaded, stored, sent, landed):
     group, me = lax.axis_index("act"), lax.axis_index("virt")
     count = groups * peers
     mine = group * peers + me
     barrier = pltpu.get_barrier_semaphore()
+    chunks = loaded.shape[1]
+    depth = trial.shape[0] // chunks
+    rows, width = trial.shape[1], trial.shape[2]
+    tail = left.shape[2]
+    cut = width - tail
+
+    def span(c):
+        return pl.ds(c * depth, depth)
+
+    def load(c, which):
+        source, target = ((trial_ref, trial), (image_ref, image), (left_ref, left), (rest_ref, rest))[which]
+        return pltpu.make_async_copy(source.at[span(c)], target.at[span(c)], loaded.at[which, c])
+
+    def load_all(c, carry):
+        for which in range(4):
+            load(c, which).start()
+        return carry
+
+    lax.fori_loop(0, chunks, load_all, 0)
 
     def target(step):
         other = lax.rem(mine + step, count)
@@ -269,52 +289,114 @@
         return carry
 
     lax.fori_loop(1, count, greet, 0)
+
+    def product(c, carry):
+        numer, denom = carry
+        for which in range(4):
+            load(c, which).wait()
+        own = image[span(c)].reshape(depth * rows, width)
+        total = jnp.dot(own, fock_ref[...], preferred_element_type=jnp.float32)
+        total += rest[span(c)].reshape(depth * rows, width).astype(jnp.float32)
+        last = total[:, cut:] + left[span(c)].reshape(depth * rows, tail).astype(jnp.float32)
+        total = jnp.concatenate([total[:, :cut], last], axis=1)
+        sigma[span(c)] = total.reshape(depth, rows, width)
+        wide = trial[span(c)].reshape(depth * rows, width).astype(jnp.float32)
+        numer += jnp.sum(wide * total, axis=0, keepdims=True)
+        denom += jnp.sum(wide * own.astype(jnp.float32), axis=0, keepdims=True)
+        return numer, denom
+
+    zero = jnp.zeros((1, width), jnp.float32)
+    numer, denom = lax.fori_loop(0, chunks, product, (zero, zero))
     pl.semaphore_wait(barrier, count - 1)
 
-    def copy(step, slot):
-        other, place = target(step)
-        return pltpu.make_async_remote_copy(
-            src_ref=part_ref, dst_ref=slots.at[slot], send_sem=sent.at[other], recv_sem=landed.at[slot],
-            device_id=place, device_id_type=MESH)
-
-    def send(step, carry):
-        copy(step, mine).start()
-        return carry
-
-    lax.fori_loop(1, count, send, 0)
-    slots[mine] = part_ref[...]
-
-    def receive(step, carry):
-        copy(step, target(step)[0]).wait_recv()
-        return carry
-
-    lax.fori_loop(1, count, receive, 0)
-    total_ref[...] = jnp.sum(slots[...], axis=0)
-
-    def finish(step, carry):
-        copy(step, mine).wait_send()
-        return carry
-
-    lax.fori_loop(1, count, finish, 0)
-
-
-def sum_all(values, groups, peers, number):
-    part = jnp.zeros((8, 128), jnp.float32)
-    for at, value in enumerate(values):
-        part = part.at[at].set(value)
-    total = pl.pallas_call(
-        functools.partial(sum_kernel, groups, peers),
-        out_shape=jax.ShapeDtypeStruct(part.shape, jnp.float32),
-        in_specs=[pl.BlockSpec(memory_space=pltpu.VMEM)],
-        out_specs=pl.BlockSpec(memory_space=pltpu.VMEM),
+    def sum_all(phase, value):
+        part[phase] = value
+
+        def copy(step, slot):
+            other, place = target(step)
+            return pltpu.make_async_remote_copy(
+                src_ref=part.at[phase], dst_ref=slots.at[phase, slot],
+                send_sem=sent.at[phase, other], recv_sem=landed.at[phase, slot],
+                device_id=place, device_id_type=MESH)
+
+        def send(step, carry):
+            copy(step, mine).start()
+            return carry
+
+        lax.fori_loop(1, count, send, 0)
+        slots[phase, mine] = value
+
+        def receive(step, carry):
+            copy(step, target(step)[0]).wait_recv()
+            return carry
+
+        lax.fori_loop(1, count, receive, 0)
+
+        def finish(step, carry):
+            copy(step, mine).wait_send()
+            return carry
+
+        lax.fori_loop(1, count, finish, 0)
+        return jnp.sum(slots[phase], axis=0)
+
+    row = lax.broadcasted_iota(jnp.int32, (8, 128), 0)
+    numer_one = jnp.sum(numer, axis=1, keepdims=True)
+    denom_one = jnp.sum(denom, axis=1, keepdims=True)
+    sums = sum_all(0, jnp.where(row == 0, numer_one, denom_one))
+    denominator = sums[1:2, 0:1]
+    rayleigh = sums[0:1, 0:1] / denominator
+
+    def store(c):
+        return pltpu.make_async_copy(rest.at[span(c)], out_ref.at[span(c)], stored.at[c])
+
+    def residual(c, squares):
+        own = image[span(c)].reshape(depth * rows, width).astype(jnp.float32)
+        resid = sigma[span(c)].reshape(depth * rows, width) - rayleigh * own
+        rest[span(c)] = resid.astype(jnp.bfloat16).reshape(depth, rows, width)
+        store(c).start()
+        return squares + jnp.sum(resid * resid, axis=0, keepdims=True)
+
+    squares = lax.fori_loop(0, chunks, residual, zero)
+    square_one = jnp.sum(squares, axis=1, keepdims=True)
+    norms = sum_all(1, jnp.broadcast_to(square_one, (8, 128)))
+    stats_ref[...] = jnp.where(row == 0, rayleigh, norms / denominator)
+
+    def drain(c, carry):
+        store(c).wait()
+        return carry
+
+    lax.fori_loop(0, chunks, drain, 0)
+
+
+def finish(groups, peers, fock, trial, image, left, rest):
+    pairs, rows, width = trial.shape
+    depth = next(d for d in (5, 4, 2, 1) if pairs % d == 0)
+    chunks = pairs // depth
+    whole = pl.BlockSpec(memory_space=pltpu.VMEM)
+    anywhere = pl.BlockSpec(memory_space=pl.ANY)
+    dma = pltpu.SemaphoreType.DMA
+    count = groups * peers
+    return pl.pallas_call(
+        functools.partial(finish_kernel, groups, peers),
+        out_shape=[
+            jax.ShapeDtypeStruct((pairs, rows, width), jnp.bfloat16),
+            jax.ShapeDtypeStruct((8, 128), jnp.float32),
+        ],
+        in_specs=[whole] + [anywhere] * 4,
+        out_specs=[anywhere, whole],
         scratch_shapes=[
-            pltpu.VMEM((groups * peers, *part.shape), jnp.float32),
-            pltpu.SemaphoreType.DMA((groups * peers,)),
-            pltpu.SemaphoreType.DMA((groups * peers,)),
+            pltpu.VMEM((pairs, rows, width), jnp.bfloat16),
+            pltpu.VMEM((pairs, rows, width), jnp.bfloat16),
+            pltpu.VMEM((pairs, rows, left.shape[2]), jnp.bfloat16),
+            pltpu.VMEM((pairs, rows, width), jnp.bfloat16),
+            pltpu.VMEM((pairs, rows, width), jnp.float32),
+            pltpu.VMEM((2, 8, 128), jnp.float32),
+            pltpu.VMEM((2, count, 8, 128), jnp.float32),
+            dma((4, chunks)), dma((chunks,)), dma((2, count)), dma((2, count)),
         ],
-        compiler_params=pltpu.CompilerParams(collective_id=number, has_side_effects=True),
-    )(part)
-    return [total[at, 0] for at in range(len(values))]
+        compiler_params=pltpu.CompilerParams(
+            collective_id=3, has_side_effects=True, vmem_limit_bytes=63 * 2**20),
+    )(fock, trial, image, left, rest)
 
 
 def local(amplitudes, virtual_fock_block, metric, active_block):
@@ -334,7 +416,7 @@
         return jnp.pad(jnp.transpose(array, (1, 0, 2)), ((0, 0), (0, tall - pairs), (0, 0)))
 
     def turn_back(array):
-        return jnp.transpose(array, (1, 0, 2))[:pairs]
+        return jnp.transpose(array, (1, 0, 2))
 
     def pair_matrix(array):
         room = tall - pairs
@@ -349,27 +431,20 @@
             fock.reshape(peers, rows, peers, rows), ((0, 0), (0, room), (0, 0), (0, room))
         ).reshape(peers * padded, peers * padded)
     metric_parts, active_parts = pair_matrix(metric), pair_matrix(active_block)
-    shift = (2.0 / fock.shape[0]) * jnp.sum(jnp.diagonal(fock).astype(jnp.float32))
+    at = lax.broadcasted_iota(jnp.int32, fock.shape, 0)
+    across = lax.broadcasted_iota(jnp.int32, fock.shape, 1)
+    shift = (2.0 / width) * jnp.sum(jnp.where(at == across, fock.astype(jnp.float32), 0.0))
+    trial = widen(amplitudes)
     applied, weighted_turned, kept = stage(
         True, peers, groups, pairs, 0, cut, (shift.reshape(1), spread, metric_parts, active_parts),
-        None, widen(amplitudes), turn(amplitudes))
-    weighted = turn_back(weighted_turned)
+        None, trial, turn(amplitudes))
+    weighted = widen(turn_back(weighted_turned))
     left, rest_turned = stage(
         False, peers, groups, pairs, cut, width - cut, (spread, metric_parts),
-        kept, widen(weighted), turn(applied[:, :rows]))
-    rest = turn_back(rest_turned)
-    right = jnp.einsum("tac,cb->tab", weighted, fock, preferred_element_type=jnp.float32)
-    left_wide = jnp.pad(left[:, :rows], ((0, 0), (0, 0), (cut, 0)))
-    sigma = left_wide.astype(jnp.float32) + right + rest.astype(jnp.float32)
-    wide = amplitudes.astype(jnp.float32)
-    weighted_wide = weighted.astype(jnp.float32)
-    numer_local = jnp.sum(wide * sigma)
-    denom_local = jnp.sum(wide * weighted_wide)
-    numerator, denominator = sum_all((numer_local, denom_local), groups, peers, 3)
-    rayleigh = numerator / denominator
-    resid = sigma - rayleigh * weighted_wide
-    squares, = sum_all((jnp.sum(resid * resid),), groups, peers, 4)
-    return resid.astype(jnp.bfloat16), rayleigh, squares / denominator
+        kept, weighted, turn(applied[:, :rows]))
+    rest = widen(turn_back(rest_turned))
+    resid, stats = finish(groups, peers, fock, trial, weighted, left, rest)
+    return resid[:, :rows], stats[0, 0], stats[1, 0]
 
 
 def solution(mesh):

time: 623 us -> 579 us (0.929)
  matrix products: 30.6 us -> 0 us
  Pallas kernels: 503 us -> 521 us
  other arithmetic: 17.2 us -> 1.84 us
  local copies, waits for them, and re-layouts: 64.4 us -> 54 us
    dot_general x1 -> x0, matrix products: 30.6 us -> none  [local(): jnp.einsum('tac,cb->tab', weighted, fock, preferred_element_type=jnp.floa...]
    pallas_call x2 -> x1, Pallas kernels: 20.9 us -> 38.7 us  [finish(): pl.pallas_call(functools.partial(finish_kernel, groups, peers), out_shape...]
    reduce_sum x2 -> x1, other arithmetic: 17.1 us -> 1.84 us  [local(): jnp.sum(jnp.where(at == across, fock.astype(jnp.float32), 0.0))]
    slice x3 -> x1, local copies, waits for them, and re-layouts: 11.2 us -> 1.27 us  [local(): return (resid[:, :rows], stats[0, 0], stats[1, 0])]
    gather x1 -> x0, local copies, waits for them, and re-layouts: 9.77 us -> none  [local(): jnp.diagonal(fock).astype(jnp.float32)]
    unnamed x11 -> x4, local copies, waits for them, and re-layouts: 7.84 us -> 16 us
where the time goes in v3:
time: 579 us; the launch traced here: 578 us
  Pallas kernels  521 us (90%)
  local copies, waits for them, and re-layouts  54 us (9%)
    pallas_call x2, Pallas kernels, stage(): pl.pallas_call(functools.partial(stage_kernel, first, peers, groups, pair...  482 us
    pallas_call x1, Pallas kernels, finish(): pl.pallas_call(functools.partial(finish_kernel, groups, peers), out_shape...  38.7 us
    pallas_call x3, local copies, waits for them, and re-layouts, stage(): pl.pallas_call(functools.partial(stage_kernel, first, peers, groups, pair...  24.3 us
    unnamed x4, local copies, waits for them, and re-layouts  16 us

profile of v3, /device:TPU:0, one launch (start us, length us, event | category | flops | bytes accessed | tf_op | source)
XLA Modules:
  0.0 578.1 jit_solution(6728097412018624212)
XLA Ops:
  0.6 1.8 select_reduce_fusion
  3.1 1.3 reshape.22
  4.4 0.1 copy.7
  4.5 0.9 pad.15
  5.3 1.3 reshape.24
  6.6 0.1 copy.8
  6.7 0.8 pad.16
  7.5 7.2 %copy.19 = bf16[100,80,640]{2,0,1:T(8,128)(2,1)S(1)} copy(bf16[100,80,640]{2,1,0:T(8,128)(2,1)} %trial_ref.1) | data formatting | bytes 20480000 | tf_op args[0]
  14.8 4.6 pad.17.refs_5_
  19.4 280.3 %shard_map.67 = (bf16[100,80,384]{2,1,0:T(8,128)(2,1)}, bf16[80,104,640]{2,1,0:T(8,128)(2,1)}, bf16[20,4,104,640]{3,2,1,0:T(8,128)(2,1)}) custom-call(f32[1]{0:T(128)} %bitcast.refs_0_, bf16[640,640]{1,0:T(8,128)(2,1)} %fock_ref.1, bf16[4,416,104]{2,1,0:T(8,128)(2,1)} %bitcast.26, bf16[4,416,104]{2,1,0:T(8,128)(2,1)} %bitcast.28, ...), custom_call_target="tpu_custom_call" | custom-call | flops 31457280000 | bytes 419430400 | tf_op jit(solution)/shard_map/pallas_call | solution.py:237
  299.7 0.0 copy-start
  299.7 11.7 %copy.18 = bf16[80,104,640]{2,0,1:T(8,128)(2,1)} copy(bf16[80,104,640]{2,1,0:T(8,128)(2,1)} %get-tuple-element.10) | data formatting | bytes 21299200 | tf_op jit(solution)/shard_map/pallas_call | solution.py:237
  311.4 0.0 copy-done
  311.4 1.4 copy.20
  312.7 3.4 pad.18.refs_4_
  316.1 202.0 %shard_map.68 = (bf16[100,80,256]{2,1,0:T(8,128)(2,1)}, bf16[80,104,640]{2,1,0:T(8,128)(2,1)}) custom-call(bf16[640,640]{1,0:T(8,128)(2,1)} %fock_ref.1, bf16[4,416,104]{2,1,0:T(8,128)(2,1)} %bitcast.27, bf16[20,4,104,640]{3,2,1,0:T(8,128)(2,1)} %get-tuple-element.11.refs_2_, bf16[104,80,640]{2,1,0:T(8,128)(2,1)} %bitcast.22, bf16[80,104,384]{2,1,0:T(8,128)(2,1)} %pad.18.refs_4_), custom_call_target="tpu_custom_call" | custom-call | flops 20971520000 | bytes 419430400 | tf_op jit(solution)/shard_map/pallas_call | solution.py:237
  518.1 11.2 %copy.17 = bf16[80,104,640]{2,0,1:T(8,128)(2,1)} copy(bf16[80,104,640]{2,1,0:T(8,128)(2,1)} %get-tuple-element.14) | data formatting | bytes 21299200 | tf_op jit(solution)/shard_map/pallas_call | solution.py:237
  529.3 38.7 %shard_map.69 = (bf16[100,80,640]{2,1,0:T(8,128)(2,1)}, f32[8,128]{1,0:T(8,128)}) custom-call(bf16[640,640]{1,0:T(8,128)(2,1)} %fock_ref.1, bf16[100,80,640]{2,1,0:T(8,128)(2,1)} %trial_ref.1, bf16[104,80,640]{2,1,0:T(8,128)(2,1)} %bitcast.23, bf16[100,80,256]{2,1,0:T(8,128)(2,1)} %get-tuple-element.13.left_ref, bf16[104,80,640]{2,1,0:T(8,128)(2,1)} %bitcast.24), custom_call_target="tpu_custom_call" | custom-call | tf_op jit(solution)/shard_map/pallas_call | solution.py:379
  568.0 1.3 fusion
  569.3 8.8 %copy.22 = bf16[100,80,640]{2,1,0:T(8,128)(2,1)} copy(bf16[100,80,640]{2,1,0:T(8,128)(2,1)} %get-tuple-element.22) | data formatting | bytes 20480000
Async XLA Ops:
  299.7 11.7 %copy-start = (bf16[100,80,384]{2,1,0:T(8,128)(2,1)S(1)}, bf16[100,80,384]{2,1,0:T(8,128)(2,1)}, u32[]{:S(2)}) copy-start(bf16[100,80,384]{2,1,0:T(8,128)(2,1)} %get-tuple-element.12) | copy-start | bytes 18432004

commit v4 on v3

--- a/solution.py
+++ b/solution.py
@@ -14,8 +14,8 @@
 def stage_kernel(first, peers, groups, pair_count, start, *refs):
     if first:
         (shift_ref, fock_ref, metric_ref, active_ref, image_ref, rows_ref,
-         left_ref, back_ref, kept_ref) = refs[:9]
-        scratch = refs[9:]
+         left_ref, back_ref, kept_ref, early_ref) = refs[:10]
+        *scratch, early_sent, early_landed = refs[10:]
     else:
         fock_ref, metric_ref, kept_ref, image_ref, rows_ref, left_ref, back_ref = refs[:7]
         scratch = refs[7:]
@@ -35,17 +35,27 @@
             barrier, inc=1, device_id=(lax.rem(group + step, groups), me), device_id_type=MESH)
     pl.semaphore_wait(barrier, peers + groups - 2)
 
+    whole_rounds = pair_count // peers
+    spare = pair_count % peers
+    stride = peers // spare if spare and peers % spare == 0 else 1
+
+    def pair_of(r, owner):
+        return r * peers + owner - (r // whole_rounds) * (owner - owner // stride)
+
+    def owns(r, owner):
+        return (r // whole_rounds) * peers * lax.rem(owner, stride) + pair_of(r, owner) < pair_count
+
     def slab(t):
         return image_ref.at[t, :, pl.ds(start, width)]
 
     def forward(r, peer):
         return pltpu.make_async_remote_copy(
-            src_ref=slab(r * peers + peer), dst_ref=held.at[r, me],
+            src_ref=slab(pair_of(r, peer)), dst_ref=held.at[r, me],
             send_sem=sent.at[r, peer], recv_sem=landed.at[r, me],
             device_id=(group, peer), device_id_type=MESH)
 
     def forward_own(r):
-        return pltpu.make_async_copy(slab(r * peers + me), held.at[r, me], landed.at[r, me])
+        return pltpu.make_async_copy(slab(pair_of(r, me)), held.at[r, me], landed.at[r, me])
 
     def arrival(r, peer):
         return pltpu.make_async_remote_copy(
@@ -55,16 +65,16 @@
 
     def backward(r, peer):
         return pltpu.make_async_remote_copy(
-            src_ref=made.at[r, peer], dst_ref=left_ref.at[r * peers + me],
+            src_ref=made.at[r, peer], dst_ref=left_ref.at[pair_of(r, me)],
             send_sem=back_sent.at[r, peer], recv_sem=back_landed.at[r, me],
             device_id=(group, peer), device_id_type=MESH)
 
     def backward_own(r):
-        return pltpu.make_async_copy(made.at[r, me], left_ref.at[r * peers + me], back_landed.at[r, me])
+        return pltpu.make_async_copy(made.at[r, me], left_ref.at[pair_of(r, me)], back_landed.at[r, me])
 
     def back_arrival(r, peer):
         return pltpu.make_async_remote_copy(
-            src_ref=made.at[r, peer], dst_ref=left_ref.at[r * peers + peer],
+            src_ref=made.at[r, peer], dst_ref=left_ref.at[pair_of(r, peer)],
             send_sem=back_sent.at[r, peer], recv_sem=back_landed.at[r, peer],
             device_id=(group, peer), device_id_type=MESH)
 
@@ -100,11 +110,32 @@
             send_sem=row_back_sent.at[i, peer], recv_sem=row_back_landed.at[i, peer],
             device_id=(peer, me), device_id_type=MESH)
 
+    if first:
+        early_width = early_ref.shape[2]
+        early_columns = pl.ds(kept_ref.shape[3] - early_width, early_width)
+
+        def early(i, peer):
+            return pltpu.make_async_remote_copy(
+                src_ref=kept_ref.at[i, peer, :, early_columns], dst_ref=early_ref.at[group * items + i],
+                send_sem=early_sent.at[i, peer], recv_sem=early_landed.at[i, group],
+                device_id=(peer, me), device_id_type=MESH)
+
+        def early_own(i):
+            return pltpu.make_async_copy(
+                kept_ref.at[i, group, :, early_columns], early_ref.at[group * items + i],
+                early_landed.at[i, group])
+
+        def early_arrival(i, peer):
+            return pltpu.make_async_remote_copy(
+                src_ref=kept_ref.at[i, peer, :, early_columns], dst_ref=early_ref.at[peer * items + i],
+                send_sem=early_sent.at[i, peer], recv_sem=early_landed.at[i, peer],
+                device_id=(peer, me), device_id_type=MESH)
+
     def launch(r):
         for step in range(peers):
             peer = lax.rem(me + step, peers)
 
-            @pl.when(r * peers + peer < pair_count)
+            @pl.when(owns(r, peer))
             def _(step=step, peer=peer):
                 if step == 0:
                     forward_own(r).start()
@@ -129,24 +160,27 @@
         total = jnp.dot(matrix_ref[0], row_held[i, 0], preferred_element_type=jnp.float32)
         for q in range(1, groups):
             total += jnp.dot(matrix_ref[q], row_held[i, q], preferred_element_type=jnp.float32)
-        return total
+        return total.reshape(groups, -1, total.shape[1])[:, :row_held.shape[2]]
 
     def mix_row(i, carry):
         row_forward_own(i).wait()
         for step in range(1, groups):
             row_arrival(i, lax.rem(group + step, groups)).wait_recv()
-        tall = row_held.shape[2]
         weighted = mix(metric_ref, i)
         if first:
             half = weighted.astype(jnp.bfloat16)
-            row_made[i] = half.reshape(groups, tall, -1)
+            row_made[i] = half
             active = mix(active_ref, i) - shift_ref[0] * (weighted - half.astype(jnp.float32))
-            kept_ref[i] = active.astype(jnp.bfloat16).reshape(groups, tall, -1)
+            kept_ref[i] = active.astype(jnp.bfloat16)
+            early_own(i).start()
+            for step in range(1, groups):
+                early(i, lax.rem(group + step, groups)).start()
         else:
-            wide = row_held.shape[3]
+            wide, part = row_held.shape[3], row_made.shape[3]
             kept = kept_ref[i, :, :, :wide].astype(jnp.float32)
-            row_made[i, :, :, :wide] = (kept + weighted.reshape(groups, tall, wide)).astype(jnp.bfloat16)
-            row_made[i, :, :, wide:] = kept_ref[i, :, :, wide:]
+            row_made[i, :, :, :wide] = (kept + weighted).astype(jnp.bfloat16)
+            if part > wide:
+                row_made[i, :, :, wide:] = kept_ref[i, :, :, wide:part]
         row_backward_own(i).start()
         for step in range(1, groups):
             row_backward(i, lax.rem(group + step, groups)).start()
@@ -159,7 +193,7 @@
 
         lax.fori_loop(jnp.minimum(r * per_step, items), jnp.minimum((r + 1) * per_step, items), mix_row, 0)
 
-        @pl.when(r * peers + me < pair_count)
+        @pl.when(owns(r, me))
         def _():
             forward_own(r).wait()
             for step in range(1, peers):
@@ -176,7 +210,7 @@
     lax.fori_loop(0, rounds, body, 0)
 
     def drain(r, carry):
-        mine = r * peers + me < pair_count
+        mine = owns(r, me)
 
         @pl.when(mine)
         def _():
@@ -185,7 +219,7 @@
         for step in range(1, peers):
             peer = lax.rem(me + step, peers)
 
-            @pl.when(r * peers + peer < pair_count)
+            @pl.when(owns(r, peer))
             def _(peer=peer):
                 forward(r, peer).wait_send()
                 back_arrival(r, peer).wait_recv()
@@ -205,12 +239,17 @@
             row_forward(i, peer).wait_send()
             row_back_arrival(i, peer).wait_recv()
             row_backward(i, peer).wait_send()
+            if first:
+                early_arrival(i, peer).wait_recv()
+                early(i, peer).wait_send()
+        if first:
+            early_own(i).wait()
         return carry
 
     lax.fori_loop(0, items, drain_row, 0)
 
 
-def stage(first, peers, groups, pairs, start, width, smalls, kept, image, turned):
+def stage(first, peers, groups, pairs, start, width, tail, smalls, kept, image, turned):
     fock = smalls[1] if first else smalls[0]
     padded = image.shape[1]
     count, tall, row_width = turned.shape
@@ -219,16 +258,18 @@
     full = image.shape[2]
     whole = pl.BlockSpec(memory_space=pltpu.VMEM)
     anywhere = pl.BlockSpec(memory_space=pl.ANY)
-    made_rows = (items, groups, tall, full)
+    kept_rows = (items, groups, tall, full)
+    made_width = full if first else full - tail
     out_shape = [
         jax.ShapeDtypeStruct((pairs, padded, width), jnp.bfloat16),
-        jax.ShapeDtypeStruct((count, tall, full), jnp.bfloat16),
+        jax.ShapeDtypeStruct((count, tall, made_width), jnp.bfloat16),
     ]
     out_specs = [anywhere, anywhere]
     if first:
         in_specs = [pl.BlockSpec(memory_space=pltpu.SMEM)] + [whole] * 3
-        out_shape.append(jax.ShapeDtypeStruct(made_rows, jnp.bfloat16))
-        out_specs.append(whole)
+        out_shape.append(jax.ShapeDtypeStruct(kept_rows, jnp.bfloat16))
+        out_shape.append(jax.ShapeDtypeStruct((count, tall, tail), jnp.bfloat16))
+        out_specs += [whole, anywhere]
         operands = smalls
     else:
         in_specs = [whole] * 3
@@ -243,10 +284,10 @@
             pltpu.VMEM((rounds, peers, padded, width), jnp.bfloat16),
             pltpu.VMEM((rounds, peers, padded, width), jnp.bfloat16),
             pltpu.VMEM((items, groups, tall, row_width), jnp.bfloat16),
-            pltpu.VMEM(made_rows, jnp.bfloat16),
+            pltpu.VMEM((items, groups, tall, made_width), jnp.bfloat16),
             dma((rounds, peers)), dma((rounds, peers)), dma((rounds, peers)), dma((rounds, peers)),
             dma((items, groups)), dma((items, groups)), dma((items, groups)), dma((items, groups)),
-        ],
+        ] + [dma((items, groups))] * (2 if first else 0),
         compiler_params=pltpu.CompilerParams(
             collective_id=1 if first else 2, has_side_effects=True, vmem_limit_bytes=60 * 2**20),
         cost_estimate=pl.CostEstimate(
@@ -254,7 +295,7 @@
     )(*operands, image, turned)
 
 
-def finish_kernel(groups, peers, fock_ref, trial_ref, image_ref, left_ref, rest_ref, out_ref, stats_ref,
+def finish_kernel(groups, peers, fock_ref, trial_ref, image_ref, left_ref, rest_ref, early_ref, out_ref, stats_ref,
                   trial, image, left, rest, sigma, part, slots, loaded, stored, sent, landed):
     group, me = lax.axis_index("act"), lax.axis_index("virt")
     count = groups * peers
@@ -270,12 +311,22 @@
         return pl.ds(c * depth, depth)
 
     def load(c, which):
-        source, target = ((trial_ref, trial), (image_ref, image), (left_ref, left), (rest_ref, rest))[which]
+        source, target = ((trial_ref, trial), (image_ref, image), (left_ref, left))[which]
         return pltpu.make_async_copy(source.at[span(c)], target.at[span(c)], loaded.at[which, c])
 
+    def load_rest(c):
+        head = rest_ref.shape[2]
+        return (
+            pltpu.make_async_copy(
+                rest_ref.at[span(c)], rest.at[span(c), :, pl.ds(0, head)], loaded.at[3, c]),
+            pltpu.make_async_copy(
+                early_ref.at[span(c)], rest.at[span(c), :, pl.ds(head, width - head)], loaded.at[4, c]))
+
     def load_all(c, carry):
-        for which in range(4):
+        for which in range(3):
             load(c, which).start()
+        for copy in load_rest(c):
+            copy.start()
         return carry
 
     lax.fori_loop(0, chunks, load_all, 0)
@@ -292,8 +343,10 @@
 
     def product(c, carry):
         numer, denom = carry
-        for which in range(4):
+        for which in range(3):
             load(c, which).wait()
+        for copy in load_rest(c):
+            copy.wait()
         own = image[span(c)].reshape(depth * rows, width)
         total = jnp.dot(own, fock_ref[...], preferred_element_type=jnp.float32)
         total += rest[span(c)].reshape(depth * rows, width).astype(jnp.float32)
@@ -368,7 +421,7 @@
     lax.fori_loop(0, chunks, drain, 0)
 
 
-def finish(groups, peers, fock, trial, image, left, rest):
+def finish(groups, peers, fock, trial, image, left, rest, early):
     pairs, rows, width = trial.shape
     depth = next(d for d in (5, 4, 2, 1) if pairs % d == 0)
     chunks = pairs // depth
@@ -382,7 +435,7 @@
             jax.ShapeDtypeStruct((pairs, rows, width), jnp.bfloat16),
             jax.ShapeDtypeStruct((8, 128), jnp.float32),
         ],
-        in_specs=[whole] + [anywhere] * 4,
+        in_specs=[whole] + [anywhere] * 5,
         out_specs=[anywhere, whole],
         scratch_shapes=[
             pltpu.VMEM((pairs, rows, width), jnp.bfloat16),
@@ -392,11 +445,11 @@
             pltpu.VMEM((pairs, rows, width), jnp.float32),
             pltpu.VMEM((2, 8, 128), jnp.float32),
             pltpu.VMEM((2, count, 8, 128), jnp.float32),
-            dma((4, chunks)), dma((chunks,)), dma((2, count)), dma((2, count)),
+            dma((5, chunks)), dma((chunks,)), dma((2, count)), dma((2, count)),
         ],
         compiler_params=pltpu.CompilerParams(
             collective_id=3, has_side_effects=True, vmem_limit_bytes=63 * 2**20),
-    )(fock, trial, image, left, rest)
+    )(fock, trial, image, left, rest, early)
 
 
 def local(amplitudes, virtual_fock_block, metric, active_block):
@@ -404,7 +457,7 @@
     peers, groups = lax.axis_size("virt"), lax.axis_size("act")
     fock = virtual_fock_block
     padded = -(-rows // 16) * 16
-    tall = -(-pairs // 8) * 8
+    room = -pairs % 8
     cut = (3 * width // 5) // 128 * 128
 
     def widen(array):
@@ -413,37 +466,37 @@
         return jnp.pad(array, ((0, 0), (0, padded - rows), (0, 0)))
 
     def turn(array):
-        return jnp.pad(jnp.transpose(array, (1, 0, 2)), ((0, 0), (0, tall - pairs), (0, 0)))
+        return jnp.transpose(array, (1, 0, 2))
 
     def turn_back(array):
         return jnp.transpose(array, (1, 0, 2))
 
     def pair_matrix(array):
-        room = tall - pairs
-        spread = jnp.pad(
-            array.reshape(groups, pairs, groups, pairs), ((0, 0), (0, room), (0, 0), (0, room)))
-        return jnp.transpose(spread, (2, 0, 1, 3)).reshape(groups, groups * tall, tall)
+        spread = jnp.pad(array.reshape(groups, pairs, groups, pairs), ((0, 0), (0, room), (0, 0), (0, 0)))
+        return jnp.transpose(spread, (2, 0, 1, 3)).reshape(groups, groups * (pairs + room), pairs)
 
     spread = fock
     if padded != rows:
-        room = padded - rows
+        gap = padded - rows
         spread = jnp.pad(
-            fock.reshape(peers, rows, peers, rows), ((0, 0), (0, room), (0, 0), (0, room))
+            fock.reshape(peers, rows, peers, rows), ((0, 0), (0, gap), (0, 0), (0, gap))
         ).reshape(peers * padded, peers * padded)
     metric_parts, active_parts = pair_matrix(metric), pair_matrix(active_block)
     at = lax.broadcasted_iota(jnp.int32, fock.shape, 0)
     across = lax.broadcasted_iota(jnp.int32, fock.shape, 1)
     shift = (2.0 / width) * jnp.sum(jnp.where(at == across, fock.astype(jnp.float32), 0.0))
     trial = widen(amplitudes)
-    applied, weighted_turned, kept = stage(
-        True, peers, groups, pairs, 0, cut, (shift.reshape(1), spread, metric_parts, active_parts),
+    tail = min(128, width - cut)
+    applied, weighted_turned, kept, early_turned = stage(
+        True, peers, groups, pairs, 0, cut, tail, (shift.reshape(1), spread, metric_parts, active_parts),
         None, trial, turn(amplitudes))
     weighted = widen(turn_back(weighted_turned))
     left, rest_turned = stage(
-        False, peers, groups, pairs, cut, width - cut, (spread, metric_parts),
+        False, peers, groups, pairs, cut, width - cut, tail, (spread, metric_parts),
         kept, weighted, turn(applied[:, :rows]))
     rest = widen(turn_back(rest_turned))
-    resid, stats = finish(groups, peers, fock, trial, weighted, left, rest)
+    early = widen(turn_back(early_turned))
+    resid, stats = finish(groups, peers, fock, trial, weighted, left, rest, early)
     return resid[:, :rows], stats[0, 0], stats[1, 0]
 
 

time: 579 us -> 572 us (0.988)
  Pallas kernels: 521 us -> 515 us
    pad x2 -> x0, local copies, waits for them, and re-layouts: 8.02 us -> none  [turn(): jnp.pad(jnp.transpose(array, (1, 0, 2)), ((0, 0), (0, tall - pairs), (0,...]
    pallas_call x2, Pallas kernels: 482 us -> 475 us  [stage(): pl.pallas_call(functools.partial(stage_kernel, first, peers, groups, pair...]
    pallas_call x3 -> x4, local copies, waits for them, and re-layouts: 24.3 us -> 27.4 us  [stage(): pl.pallas_call(functools.partial(stage_kernel, first, peers, groups, pair...]
where the time goes in v4:
time: 572 us; the launch traced here: 571 us
  Pallas kernels  515 us (90%)
  local copies, waits for them, and re-layouts  53.4 us (9%)
    pallas_call x2, Pallas kernels, stage(): pl.pallas_call(functools.partial(stage_kernel, first, peers, groups, pair...  475 us
    pallas_call x1, Pallas kernels, finish(): pl.pallas_call(functools.partial(finish_kernel, groups, peers), out_shape...  40 us
    pallas_call x4, local copies, waits for them, and re-layouts, stage(): pl.pallas_call(functools.partial(stage_kernel, first, peers, groups, pair...  27.4 us
    unnamed x4, local copies, waits for them, and re-layouts  20.3 us

profile of v4, /device:TPU:0, one launch (start us, length us, event | category | flops | bytes accessed | tf_op | source)
XLA Modules:
  0.0 571.2 jit_solution(9776829869237930080)
XLA Ops:
  0.6 1.8 select_reduce_fusion
  3.1 1.3 reshape.22
  4.4 0.1 copy.7
  4.5 0.9 pad.7
  5.3 1.3 reshape.24
  6.6 0.1 copy.8
  6.7 0.8 pad.8
  7.5 11.5 %copy.19 = bf16[100,80,640]{2,0,1:T(8,128)(2,1)} copy(bf16[100,80,640]{2,1,0:T(8,128)(2,1)} %trial_ref.1) | data formatting | bytes 20480000 | tf_op args[0]
  19.0 282.8 %shard_map.67 = (bf16[100,80,384]{2,1,0:T(8,128)(2,1)}, bf16[80,100,640]{2,1,0:T(8,128)(2,1)}, bf16[20,4,100,640]{3,2,1,0:T(8,128)(2,1)}, bf16[80,100,128]{2,1,0:T(8,128)(2,1)}) custom-call(f32[1]{0:T(128)} %bitcast.refs_0_, bf16[640,640]{1,0:T(8,128)(2,1)} %fock_ref.1, bf16[4,416,100]{2,1,0:T(8,128)(2,1)} %bitcast.30, bf16[4,416,100]{2,1,0:T(8,128)(2,1)} %bitcast.32, ...), custom_call_target="tpu_custom_call" | custom-call | flops 31457280000 | bytes 419430400 | tf_op jit(solution)/shard_map/pallas_call | solution.py:278
  301.8 0.0 copy-start
  301.8 9.5 %copy.20 = bf16[80,100,640]{2,0,1:T(8,128)(2,1)} copy(bf16[80,100,640]{2,1,0:T(8,128)(2,1)} %get-tuple-element.11) | data formatting | bytes 20480000 | tf_op jit(solution)/shard_map/pallas_call | solution.py:278
  311.3 0.0 copy-done
  311.3 1.6 copy.23
  312.9 6.8 %copy.22 = bf16[100,80,384]{2,0,1:T(8,128)(2,1)} copy(bf16[100,80,384]{2,1,0:T(8,128)(2,1)} %get-tuple-element.13) | data formatting | bytes 12288000 | tf_op jit(solution)/shard_map/pallas_call | solution.py:278
  319.7 191.8 %shard_map.68 = (bf16[100,80,256]{2,1,0:T(8,128)(2,1)}, bf16[80,100,512]{2,1,0:T(8,128)(2,1)}) custom-call(bf16[640,640]{1,0:T(8,128)(2,1)} %fock_ref.1, bf16[4,416,100]{2,1,0:T(8,128)(2,1)} %bitcast.31, bf16[20,4,100,640]{3,2,1,0:T(8,128)(2,1)} %get-tuple-element.12.refs_2_, bf16[100,80,640]{2,1,0:T(8,128)(2,1)} %bitcast.24, bf16[80,100,384]{2,1,0:T(8,128)(2,1)} %bitcast.29), custom_call_target="tpu_custom_call" | custom-call | flops 20971520000 | bytes 419430400 | tf_op jit(solution)/shard_map/pallas_call | solution.py:278
  511.5 9.6 %copy.21 = bf16[80,100,512]{2,0,1:T(8,128)(2,1)} copy(bf16[80,100,512]{2,1,0:T(8,128)(2,1)} %get-tuple-element.15) | data formatting | bytes 16384000 | tf_op jit(solution)/shard_map/pallas_call | solution.py:278
  521.1 40.0 %shard_map.69 = (bf16[100,80,640]{2,1,0:T(8,128)(2,1)}, f32[8,128]{1,0:T(8,128)}) custom-call(bf16[640,640]{1,0:T(8,128)(2,1)} %fock_ref.1, bf16[100,80,640]{2,1,0:T(8,128)(2,1)} %trial_ref.1, bf16[100,80,640]{2,1,0:T(8,128)(2,1)} %bitcast.25, bf16[100,80,256]{2,1,0:T(8,128)(2,1)} %get-tuple-element.14.left_ref, bf16[100,80,512]{2,1,0:T(8,128)(2,1)} %bitcast.26, ...), custom_call_target="tpu_custom_call" | custom-call | tf_op jit(solution)/shard_map/pallas_call | solution.py:432
  561.2 1.3 fusion
  562.5 8.8 %copy.25 = bf16[100,80,640]{2,1,0:T(8,128)(2,1)} copy(bf16[100,80,640]{2,1,0:T(8,128)(2,1)} %get-tuple-element.24) | data formatting | bytes 20480000
Async XLA Ops:
  301.8 9.5 %copy-start = (bf16[80,100,128]{2,1,0:T(8,128)(2,1)S(1)}, bf16[80,100,128]{2,1,0:T(8,128)(2,1)}, u32[]{:S(2)}) copy-start(bf16[80,100,128]{2,1,0:T(8,128)(2,1)} %get-tuple-element.16) | copy-start | bytes 6144004
